TPU v7x, 512 devices: a 8x2x16 block of a 8x8x16 slice. The times are simulated.
512 devices in a mesh: member: 2 (over y), seq: 16 (over z), dp: 8 (over x), mp: 2 (over core).
Axes of the slice: x: 8, y: 2, z: 16, core: 2. Of those that a mesh axis runs over, the one named last changes fastest.
The devices are a block of a 8x8x16 slice.
Arguments:
- mixer_in: bfloat16 [16, 2048, 3072], P(('member', 'dp'), 'seq', 'mp'), parts along dimension 0, may hold values from -6 to 6
- delta_raw: bfloat16 [16, 2048, 3072], P(('member', 'dp'), 'seq', 'mp'), parts along dimension 0, may hold values from -2 to 2048
- delta_bias: float32 [6144], P(('member', 'mp')), parts along dimension 0, may hold values from -4 to -2
- decay_log: float32 [6144, 16], P(('member', 'mp')), parts along dimension 0, may hold values from -12 to 1
- skip_gain: float32 [6144], P(('member', 'mp')), parts along dimension 0, may hold values from 0.5 to 1.5
- state_write: bfloat16 [16, 2048, 16], P(('member', 'dp'), 'seq'), parts along dimension 0, may hold values from -5 to 5
- state_read: bfloat16 [16, 2048, 16], P(('member', 'dp'), 'seq'), parts along dimension 0, may hold values from -1.5 to 1.5
- mixer_grad: bfloat16 [16, 2048, 3072], P(('member', 'dp'), 'seq', 'mp'), parts along dimension 0, may hold values from -6 to 6
- attn_query: bfloat16 [16, 2048, 1536], P(('member', 'dp'), 'seq', 'mp'), parts along dimension 0, may hold values from -5 to 5
- attn_key: bfloat16 [16, 2048, 1536], P(('member', 'dp'), 'seq', 'mp'), parts along dimension 0, may hold values from -5 to 5
- attn_value: bfloat16 [16, 2048, 1536], P(('member', 'dp'), 'seq', 'mp'), parts along dimension 0, may hold values from -6 to 6
- attn_grad: bfloat16 [16, 2048, 1536], P(('member', 'dp'), 'seq', 'mp'), parts along dimension 0, may hold values from -6 to 6
- document_id: int32 [16, 2048], P(('member', 'dp'), 'seq'), parts along dimension 0, may hold values from 0 to 3, never falling along the last dimension, each value on 1 to 1024 neighbouring positions
Outputs:
- mixer_out: bfloat16 [16, 2048, 3072], P(('member', 'dp'), 'seq', 'mp'), parts along dimension 0
- input_grad: bfloat16 [16, 2048, 3072], P(('member', 'dp'), 'seq', 'mp'), parts along dimension 0
- delta_grad: bfloat16 [16, 2048, 3072], P(('member', 'dp'), 'seq', 'mp'), parts along dimension 0
- decay_grad: float32 [6144, 16], P(('member', 'mp')), parts along dimension 0
- skip_grad: float32 [6144], P(('member', 'mp')), parts along dimension 0
- bias_grad: float32 [6144], P(('member', 'mp')), parts along dimension 0
- attn_out: bfloat16 [16, 2048, 1536], P(('member', 'dp'), 'seq', 'mp'), parts along dimension 0
- query_grad: bfloat16 [16, 2048, 1536], P(('member', 'dp'), 'seq', 'mp'), parts along dimension 0
- key_grad: bfloat16 [16, 2048, 1536], P(('member', 'dp'), 'seq', 'mp'), parts along dimension 0
- value_grad: bfloat16 [16, 2048, 1536], P(('member', 'dp'), 'seq', 'mp'), parts along dimension 0
There are 2 independent parts, one for each index of `member`. A program takes and returns all parts, laid end to end along the dimension named above; each array names one. Nothing has to cross between parts.
Inputs may be any that keep to these rules, and one draw needn't show every extreme that they name: `document_id`: document numbers never fall along a sequence; a document covers at most 1024 positions.
All inputs are finite; a program needn't handle non-finite values.
Results may differ from a plain program's by a relative error of at most 0.024.
Values may be sent and summed in bfloat16 or wider, within the bound.
A program may use at most 128 MiB of HBM per device.

v0:
```python
import functools
import math

import jax
import jax.numpy as jnp
from jax import lax
from jax.sharding import PartitionSpec as P

HD = 96
WINDOW = 128


neg_large = -1e30
unroll_steps = 8


def prefix_2(x, axis, combine, identity, reverse):
    count, position = (lax.axis_size(axis), lax.axis_index(axis))
    everything = jax.tree.map(lambda part: lax.all_gather(part, axis), x)
    start = jax.tree.map(
        lambda part, zero: jnp.broadcast_to(jnp.asarray(zero, part.dtype), part.shape), x, identity
    )

    def lap(k, before):
        at = count - 1 - k if reverse else k
        reached = at > position if reverse else at < position
        new = combine(before, jax.tree.map(lambda part: part[at], everything))
        return jax.tree.map(lambda a, b: jnp.where(reached, a, b), new, before)

    return lax.fori_loop(0, count, lap, start)


def one_axis_at_a_time(x, axes):
    return functools.reduce(lax.psum, axes, x)


def shifted(value, axis, steps):
    count = lax.axis_size(axis)
    leading, last = (max(0, -steps), min(count, count - steps))
    return lax.ppermute(value, axis, [(source, source + steps) for source in range(leading, last)])


def compose(earlier, later):
    return (earlier[0] * later[0], later[1] + later[0] * earlier[1])


def summaries(step_size, weighted, writes, reads, grads, rate):
    prefix = jnp.cumsum(step_size, axis=0)
    total = prefix[-1]
    suffix = total[None, :] - prefix
    through = jnp.exp(rate * total[:, None])
    ending = jnp.sum(
        weighted[:, :, None] * writes[:, None, :] * jnp.exp(suffix[:, :, None] * rate[None]), axis=0
    )
    leading = jnp.sum(
        grads[:, :, None] * reads[:, None, :] * jnp.exp(prefix[:, :, None] * rate[None]), axis=0
    )
    return (through, ending, leading)


def run_forward(start, step_size, weighted, writes, rate):
    count = step_size.shape[0] // unroll_steps

    def advance(state, items):
        sizes, weights, write_rows = items
        outputs = []
        for position in range(unroll_steps):
            state = (
                jnp.exp(sizes[position][:, None] * rate) * state
                + weights[position][:, None] * write_rows[position][None, :]
            )
            outputs.append(state)
        return (state, jnp.stack(outputs))

    shaped = (
        step_size.reshape(count, unroll_steps, -1),
        weighted.reshape(count, unroll_steps, -1),
        writes.reshape(count, unroll_steps, -1),
    )
    _, states = lax.scan(advance, start, shaped)
    return states.reshape((count * unroll_steps,) + start.shape)


def run_backward(start, step_size, inputs, grads, writes, reads, previous, rate, skip_gain):
    count = step_size.shape[0] // unroll_steps
    channels = step_size.shape[1]

    def retreat(carry, items):
        back, accum = carry
        sizes, values, outs, write_rows, read_rows, prior = items
        input_list = []
        step_list = []
        for position in reversed(range(unroll_steps)):
            decay = jnp.exp(sizes[position][:, None] * rate)
            adjoint = read_rows[position][None, :] * outs[position][:, None] + back
            through_write = jnp.sum(adjoint * write_rows[position][None, :], axis=1)
            input_list.append(through_write * sizes[position] + skip_gain * outs[position])
            tail = adjoint * prior[position] * decay
            step_list.append(values[position] * through_write + jnp.sum(tail * rate, axis=1))
            accum = accum + tail * sizes[position][:, None]
            back = decay * adjoint
        return ((back, accum), (jnp.stack(input_list[::-1]), jnp.stack(step_list[::-1])))

    shaped = (
        step_size.reshape(count, unroll_steps, -1),
        inputs.reshape(count, unroll_steps, -1),
        grads.reshape(count, unroll_steps, -1),
        writes.reshape(count, unroll_steps, -1),
        reads.reshape(count, unroll_steps, -1),
        previous.reshape((count, unroll_steps) + start.shape),
    )
    (_, accum), (input_grad, step_grad) = lax.scan(
        retreat, (start, jnp.zeros_like(start)), shaped, reverse=True
    )
    return (input_grad.reshape(-1, channels), step_grad.reshape(-1, channels), accum)


def body(
    mixer_in,
    delta_raw,
    delta_bias,
    decay_log,
    skip_gain,
    state_write,
    state_read,
    mixer_grad,
    attn_query,
    attn_key,
    attn_value,
    attn_grad,
    document_id,
):
    inputs = mixer_in[0].astype(jnp.float32)
    raws = delta_raw[0].astype(jnp.float32)
    grads = mixer_grad[0].astype(jnp.float32)
    writes = state_write[0].astype(jnp.float32)
    reads = state_read[0].astype(jnp.float32)
    rate = -jnp.exp(decay_log)
    step_size = jax.nn.softplus(raws + delta_bias[None, :])
    weighted = step_size * inputs
    through, ending, leading = summaries(step_size, weighted, writes, reads, grads, rate)
    zeros = jnp.zeros_like(through)
    ones = jnp.ones_like(through)
    forward_pair = prefix_2((through, ending), "seq", compose, (ones, zeros), False)
    backward_pair = prefix_2((through, leading), "seq", compose, (ones, zeros), True)
    state_start = forward_pair[1]
    adjoint_start = backward_pair[1]
    states = run_forward(state_start, step_size, weighted, writes, rate)
    mixed = jnp.sum(states * reads[:, None, :], axis=2) + skip_gain[None, :] * inputs
    previous = jnp.concatenate([state_start[None], states[:-1]], axis=0)
    input_grad, step_grad, decay_part = run_backward(
        adjoint_start, step_size, inputs, grads, writes, reads, previous, rate, skip_gain
    )
    raw_grad = step_grad * jax.nn.sigmoid(raws + delta_bias[None, :])
    sums = (
        one_axis_at_a_time(decay_part * rate, ("seq", "dp")),
        one_axis_at_a_time(jnp.sum(grads * inputs, axis=0), ("seq", "dp")),
        one_axis_at_a_time(jnp.sum(raw_grad, axis=0), ("seq", "dp")),
    )
    grad_scale = 1.0 / math.sqrt(inputs.shape[0] * lax.axis_size("seq") * lax.axis_size("dp"))
    query = attn_query[0]
    key_now = attn_key[0]
    value_now = attn_value[0]
    out_grad = attn_grad[0]
    length = query.shape[0]
    width = query.shape[1]
    heads = width // HD
    doc_now = (document_id[0] + 1).astype(jnp.bfloat16)
    key_before, value_before, doc_before = shifted((key_now, value_now, doc_now), "seq", 1)
    key_all = jnp.concatenate([key_before, key_now], axis=0).reshape(2 * length, heads, HD)
    value_all = jnp.concatenate([value_before, value_now], axis=0).reshape(2 * length, heads, HD)
    doc_all = jnp.concatenate([doc_before, doc_now], axis=0)
    query_heads = query.reshape(length, heads, HD)
    grad_heads = out_grad.reshape(length, heads, HD)
    offset = jnp.arange(length)[:, None] + length - jnp.arange(2 * length)[None, :]
    allowed = (offset >= 0) & (offset < WINDOW) & (doc_all[None, :] == doc_now[:, None])
    scale = 1.0 / math.sqrt(HD)
    scores = (
        jnp.einsum("qhd,khd->hqk", query_heads, key_all, preferred_element_type=jnp.float32) * scale
    )
    scores = jnp.where(allowed[None], scores, neg_large)
    top = jnp.max(scores, axis=2)
    log_total = top + jnp.log(jnp.sum(jnp.exp(scores - top[:, :, None]), axis=2))
    probs = jnp.exp(scores - log_total[:, :, None])
    probs_low = probs.astype(jnp.bfloat16)
    attended = jnp.einsum(
        "hqk,khd->qhd", probs_low, value_all, preferred_element_type=jnp.float32
    ).astype(jnp.bfloat16)
    row_term = jnp.einsum("qhd,qhd->hq", grad_heads, attended, preferred_element_type=jnp.float32)
    value_score = jnp.einsum(
        "qhd,khd->hqk", grad_heads, value_all, preferred_element_type=jnp.float32
    )
    score_grad = (probs * (value_score - row_term[:, :, None])).astype(jnp.bfloat16)
    query_grad = (
        jnp.einsum("hqk,khd->qhd", score_grad, key_all, preferred_element_type=jnp.float32) * scale
    ).astype(jnp.bfloat16)
    key_parts = (
        jnp.einsum("hqk,qhd->khd", score_grad, query_heads, preferred_element_type=jnp.float32)
        * scale
    ).reshape(2 * length, width)
    value_parts = jnp.einsum(
        "hqk,qhd->khd", probs_low, grad_heads, preferred_element_type=jnp.float32
    ).reshape(2 * length, width)
    key_back, value_back = shifted((key_parts[:length], value_parts[:length]), "seq", -1)
    key_total = key_parts[length:] + key_back
    value_total = value_parts[length:] + value_back
    return (
        mixed.astype(jnp.bfloat16)[None],
        input_grad.astype(jnp.bfloat16)[None],
        raw_grad.astype(jnp.bfloat16)[None],
        sums[0] * grad_scale,
        sums[1] * grad_scale,
        sums[2] * grad_scale,
        attended.reshape(length, width)[None],
        query_grad.reshape(length, width)[None],
        key_total.astype(jnp.bfloat16)[None],
        value_total.astype(jnp.bfloat16)[None],
    )


def solution(mesh):
    return jax.shard_map(
        body,
        mesh=mesh,
        in_specs=(
            P(("member", "dp"), "seq", "mp"),
            P(("member", "dp"), "seq", "mp"),
            P(("member", "mp")),
            P(("member", "mp"), None),
            P(("member", "mp")),
            P(("member", "dp"), "seq", None),
            P(("member", "dp"), "seq", None),
            P(("member", "dp"), "seq", "mp"),
            P(("member", "dp"), "seq", "mp"),
            P(("member", "dp"), "seq", "mp"),
            P(("member", "dp"), "seq", "mp"),
            P(("member", "dp"), "seq", "mp"),
            P(("member", "dp"), "seq"),
        ),
        out_specs=(
            P(("member", "dp"), "seq", "mp"),
            P(("member", "dp"), "seq", "mp"),
            P(("member", "dp"), "seq", "mp"),
            P(("member", "mp"), None),
            P(("member", "mp")),
            P(("member", "mp")),
            P(("member", "dp"), "seq", "mp"),
            P(("member", "dp"), "seq", "mp"),
            P(("member", "dp"), "seq", "mp"),
            P(("member", "dp"), "seq", "mp"),
        ),
        check_vma=False,
    )
```

profile of v0, /device:TPU:80, one launch (start us, length us, event | category | flops | bytes accessed | tf_op | source)
XLA Modules:
  0.0 758.1 jit_solution(14903778104523084410)
XLA Ops:
  8.2 2.7 convert_bitcast_fusion.4
  10.9 2.7 fusion.84
  16.8 6.9 multiply_reduce_fusion.16
  24.6 6.0 collective-permute-start.2
  30.7 6.0 collective-permute-start.1
  36.7 6.0 collective-permute-start
  65.0 10.3 %collective-permute-done.3 = f32[128,768]{1,0:T(8,128)} collective-permute-done((f32[128,768]{1,0:T(8,128)}, f32[128,768]{1,0:T(8,128)}, u32[]{:S(2)}, u32[]{:S(2)}) %collective-permute-start.3) | collective-permute-done | bytes 393248 | tf_op jit(solution)/shard_map/ppermute | solution.py:40
  77.0 7.2 collective-permute-done.4
  85.9 45.4 %all-gather.7.cloned.1.call-done = f32[24576,16]{0,1:T(8,128)} async-done(((f32[1536,16]{0,1:T(8,128)}), f32[24576,16]{0,1:T(8,128)}) %all-gather.7.cloned.1.call-update) | async-done | bytes 1572880 | tf_op jit(solution)/shard_map/all_gather | solution.py:19
  131.3 3.5 copy.112
  134.8 69.5 %all-gather.9.cloned.1.call-done = f32[24576,16]{0,1:T(8,128)} async-done(((f32[1536,16]{0,1:T(8,128)}), f32[24576,16]{0,1:T(8,128)}) %all-gather.9.cloned.1.call-update) | async-done | bytes 1572880 | tf_op jit(solution)/shard_map/all_gather | solution.py:19
  205.9 20.8 %while.64 = (s32[]{:T(128)}, f32[1536,16]{0,1:T(8,128)S(1)}, s32[]{:T(128)}, f32[16,1536,16]{1,0,2:T(8,128)}, f32[16,1536,16]{1,2,0:T(8,128)S(1)}, /*index=5*/s32[]{:T(128)}, s32[]{:T(128)}) while((s32[]{:T(128)}, f32[1536,16]{0,1:T(8,128)S(1)}, s32[]{:T(128)}, f32[16,1536,16]{1,0,2:T(8,128)}, f32[16,1536,16]{1,2,0:T(8,128)S(1)}, ...), condition=%wide.region_3.4_spmd.clone, body=%wide.region_2.3_spmd.clone.sunk | while | flops 98308 | bytes 589937 | solution.py:30
  226.7 58.0 %while.63 = (s32[]{:T(128)}, f32[1536,16]{0,1:T(8,128)S(1)}, f32[16,8,1536,16]{2,3,1,0:T(8,128)}, f32[16,8,1536]{2,1,0:T(8,128)}, f32[1536,16]{0,1:T(8,128)S(1)}...) while((s32[]{:T(128)}, f32[1536,16]{0,1:T(8,128)S(1)}, ...), condition=%wide.region_5.6_spmd, body=%wide.region_4.5_spmd.sunk | while | flops 1966088 | bytes 4661081 | solution.py:80
  226.7 1.9 dynamic-slice_reduce_fusion.17
  237.4 2.0 dynamic-slice_reduce_fusion.17
  241.2 2.0 dynamic-slice_reduce_fusion.17
  245.0 1.8 dynamic-slice_reduce_fusion.17
  248.6 1.8 dynamic-slice_reduce_fusion.17
  252.2 1.8 dynamic-slice_reduce_fusion.17
  259.3 1.8 dynamic-slice_reduce_fusion.17
  262.9 1.8 dynamic-slice_reduce_fusion.17
  266.5 1.8 dynamic-slice_reduce_fusion.17
  270.1 1.8 dynamic-slice_reduce_fusion.17
  273.7 2.0 dynamic-slice_reduce_fusion.17
  281.1 1.8 dynamic-slice_reduce_fusion.17
  284.6 3.5 copy.113
  288.1 20.7 %while.65 = (s32[]{:T(128)}, f32[1536,16]{0,1:T(8,128)S(1)}, s32[]{:T(128)}, f32[16,1536,16]{1,0,2:T(8,128)}, f32[16,1536,16]{1,2,0:T(8,128)S(1)}, /*index=5*/s32[]{:T(128)}, s32[]{:T(128)}, s32[]{:T(128)}, s32[]{:T(128)}) while((s32[]{:T(128)}, f32[1536,16]{0,1:T(8,128)S(1)}, s32[]{:T(128)}, f32[16,1536,16]{1,0,2:T(8,128)}, ...), condition=%wide.region_9.10_spmd.clone, body=%wide.region_8.9_spmd.clone.sunk | while | flops 98312 | bytes 589999 | solution.py:30
  308.8 6.9 multiply_reduce_fusion.17
  315.6 11.4 %slice.689 = f32[127,1536,16]{1,2,0:T(8,128)} slice(f32[128,1536,16]{1,2,0:T(8,128)} %bitcast.504), slice={[0:127], [0:1536], [0:16]} | slice | bytes 24969216 | tf_op jit(solution)/shard_map/slice | solution.py:150
  327.0 11.5 %pad_maximum_fusion = f32[128,1536,16]{1,2,0:T(8,128)} fusion(f32[127,1536,16]{1,2,0:T(8,128)} %slice.689, f32[1,1536,16]{1,2,0:T(8,128)S(1)} %bitcast.506), kind=kLoop, calls=%fused_computation.225 | loop fusion | flops 3145728 | bytes 25165824 | tf_op jit(solution)/shard_map/concatenate | solution.py:150
  338.6 189.0 %while.66 = (s32[]{:T(128)}, f32[1536,16]{0,1:T(8,128)S(1)}, f32[1536,16]{0,1:T(8,128)S(1)}, bf16[16,8,1536]{2,1,0:T(8,128)(2,1)}, f32[16,8,1536]{2,1,0:T(8,128)...) while((s32[]{:T(128)}, f32[1536,16]{0,1:T(8,128)S(1)}, ...), condition=%wide.region_27.28_spmd.clone, body=%wide.region_10.27_spmd.clone.sunk | while | flops 4374539 | bytes 4418103 | solution.py:112
  338.6 1.8 fusion.148
  350.4 1.8 fusion.148
  362.2 2.1 fusion.148
  369.7 1.9 fusion.150
  374.5 1.8 fusion.148
  386.3 1.8 fusion.148
  398.1 1.8 fusion.148
  409.9 1.8 fusion.148
  433.4 1.8 fusion.148
  456.9 1.8 fusion.148
  480.4 1.9 fusion.148
  504.0 1.8 fusion.148
  515.8 1.8 fusion.148
  530.5 55.3 %all-reduce = (f32[1536]{0:T(1024)S(1)}, f32[1536]{0:T(1024)S(1)}) all-reduce(f32[1536]{0:T(1024)S(1)} %get-tuple-element.859, f32[1536]{0:T(1024)S(1)} %fusion.114), channel_id=1, replica_groups=mesh['member'=2,'seq'=16,'dp'=8,'mp'=2] {'seq'}, use_global_device_ids=true, to_apply=%region_31.32 | all-reduce | flops 3072 | bytes 24576 | tf_op jit(solution)/shard_map/psum | solution.py:34
  585.8 29.6 %all-reduce.1 = (f32[1536]{0:T(1024)S(1)}, f32[1536]{0:T(1024)S(1)}) all-reduce(f32[1536]{0:T(1024)S(1)} %get-tuple-element.783, f32[1536]{0:T(1024)S(1)} %get-tuple-element.784), channel_id=1, replica_groups=mesh['member'=2,'seq'=16,'dp'=8,'mp'=2] {'dp'}, use_global_device_ids=true, to_apply=%region_32.33 | all-reduce | flops 3072 | bytes 24576 | tf_op jit(solution)/shard_map/psum | solution.py:34
  616.0 51.1 %all-reduce.5.cloned.1.call-done = f32[1536,16]{0,1:T(8,128)} async-done(((f32[1536,16]{0,1:T(8,128)}), f32[1536,16]{0,1:T(8,128)}) %all-reduce.5.cloned.1.call-update) | async-done | bytes 98320 | tf_op jit(solution)/shard_map/psum | solution.py:34
  667.8 82.2 %all-reduce.7.cloned.1.call-done = f32[1536,16]{0,1:T(8,128)} async-done(((f32[1536,16]{0,1:T(8,128)}), f32[1536,16]{0,1:T(8,128)}) %all-reduce.7.cloned.1.call-update) | async-done | bytes 98320 | tf_op jit(solution)/shard_map/psum | solution.py:34
  (593 shorter events, 276.7 us)
Async XLA Ops:
  7.2 37.6 %copy-start.8 = (bf16[1,128,16]{1,2,0:T(8,128)(2,1)S(1)}, bf16[1,128,16]{1,2,0:T(8,128)(2,1)}, u32[]{:S(2)}) copy-start(bf16[1,128,16]{1,2,0:T(8,128)(2,1)} %param.27) | copy-start | bytes 12292
  7.2 35.7 %copy-start = (bf16[1,128,1536]{2,1,0:T(8,128)(2,1)S(1)}, bf16[1,128,1536]{2,1,0:T(8,128)(2,1)}, u32[]{:S(2)}) copy-start(bf16[1,128,1536]{2,1,0:T(8,128)(2,1)} %param.21) | copy-start | bytes 1179652
  7.2 35.7 %copy-start.6 = (f32[1536]{0:T(1024)S(1)}, f32[1536]{0:T(1024)}, u32[]{:S(2)}) copy-start(f32[1536]{0:T(1024)} %param.23) | copy-start | bytes 18436
  7.2 35.7 %copy-start.1 = (bf16[1,128,1536]{2,1,0:T(8,128)(2,1)S(1)}, bf16[1,128,1536]{2,1,0:T(8,128)(2,1)}, u32[]{:S(2)}) copy-start(bf16[1,128,1536]{2,1,0:T(8,128)(2,1)} %param.22) | copy-start | bytes 1179652
  7.2 37.4 %copy-start.7 = (bf16[1,128,16]{1,2,0:T(8,128)(2,1)S(1)}, bf16[1,128,16]{1,2,0:T(8,128)(2,1)}, u32[]{:S(2)}) copy-start(bf16[1,128,16]{1,2,0:T(8,128)(2,1)} %param.26) | copy-start | bytes 12292
  7.2 23.4 %copy-start.9 = (s32[1,128]{1,0:T(1,128)S(1)}, s32[1,128]{1,0:T(1,128)}, u32[]{:S(2)}) copy-start(s32[1,128]{1,0:T(1,128)} %param.33) | copy-start | bytes 1540
  7.3 124.1 %all-gather.7.cloned.1.call-start = ((), (), s32[]{:S(2)}) async-start(), calls=%async_computation.2 | async-start | bytes 1671168 | tf_op jit(solution)/shard_map/all_gather | solution.py:19
  23.8 180.6 %all-gather.9.cloned.1.call-start = ((), (), s32[]{:S(2)}) async-start(), calls=%async_computation.3 | async-start | bytes 1671168 | tf_op jit(solution)/shard_map/all_gather | solution.py:19
  24.6 260.1 %all-gather.11.cloned.1.call-start = ((), (), s32[]{:S(2)}) async-start(), calls=%async_computation.4 | async-start | bytes 1671168 | tf_op jit(solution)/shard_map/all_gather | solution.py:19
  24.6 25.7 %collective-permute-start.2 = (bf16[128,768]{1,0:T(8,128)(2,1)}, bf16[128,768]{1,0:T(8,128)(2,1)S(1)}, u32[]{:S(2)}, u32[]{:S(2)}) collective-permute-start(bf16[128,768]{1,0:T(8,128)(2,1)} %bitcast.39), channel_id=1, source_target_pairs={{0,16},{16,32},{32,48},{48,64},{64,80},{80,96},{96,112},{112,128},... | collective-permute-start | bytes 589832 | tf_op jit(solution)/shard_map/ppermute | solution.py:40
  30.7 19.5 %collective-permute-start.1 = (bf16[128]{0:T(256)(128)(2,1)S(1)}, bf16[128]{0:T(256)(128)(2,1)S(1)}, u32[]{:S(2)}, u32[]{:S(2)}) collective-permute-start(bf16[128]{0:T(256)(128)(2,1)S(1)} %convert_bitcast_fusion.9), channel_id=1, source_target_pairs={{0,16},{16,32},{32,48},{48,64},{64,80},{80,96},{96,112},{112,128},... | collective-permute-start | bytes 776 | tf_op jit(solution)/shard_map/ppermute | solution.py:40
  36.7 15.9 %collective-permute-start = (bf16[128,768]{1,0:T(8,128)(2,1)}, bf16[128,768]{1,0:T(8,128)(2,1)S(1)}, u32[]{:S(2)}, u32[]{:S(2)}) collective-permute-start(bf16[128,768]{1,0:T(8,128)(2,1)} %bitcast.35), channel_id=1, source_target_pairs={{0,16},{16,32},{32,48},{48,64},{64,80},{80,96},{96,112},{112,128},... | collective-permute-start | bytes 589832 | tf_op jit(solution)/shard_map/ppermute | solution.py:40
  42.8 624.3 %all-reduce.5.cloned.1.call-start = ((), (), s32[]{:S(2)}) async-start(), calls=%async_computation | async-start | bytes 196608 | tf_op jit(solution)/shard_map/psum | solution.py:34
  46.8 6.0 copy-start.5
  50.2 2.5 copy-start.2
  57.8 17.5 %collective-permute-start.3 = (f32[128,768]{1,0:T(8,128)}, f32[128,768]{1,0:T(8,128)}, u32[]{:S(2)}, u32[]{:S(2)}) collective-permute-start(f32[128,768]{1,0:T(8,128)} %copy.90), channel_id=1, source_target_pairs={{16,0},{32,16},{48,32},{64,48},{80,64},{96,80},{112,96},{128,112},... | collective-permute-start | bytes 1179656 | tf_op jit(solution)/shard_map/ppermute | solution.py:40
  61.2 23.0 %collective-permute-start.4 = (f32[128,768]{1,0:T(8,128)}, f32[128,768]{1,0:T(8,128)}, u32[]{:S(2)}, u32[]{:S(2)}) collective-permute-start(f32[128,768]{1,0:T(8,128)} %copy.93), channel_id=1, source_target_pairs={{16,0},{32,16},{48,32},{64,48},{80,64},{96,80},{112,96},{128,112},... | collective-permute-start | bytes 1179656 | tf_op jit(solution)/shard_map/ppermute | solution.py:40
  327.0 11.6 %copy-start.4 = (f32[1536]{0:T(1024)S(1)}, f32[1536]{0:T(1024)}, u32[]{:S(2)}) copy-start(f32[1536]{0:T(1024)} %param.25) | copy-start | bytes 18436
  338.6 191.1 %copy-start.3 = (f32[1536,16]{0,1:T(8,128)S(1)}, f32[1536,16]{0,1:T(8,128)}, u32[]{:S(2)}) copy-start(f32[1536,16]{0,1:T(8,128)} %param.24) | copy-start | bytes 294916
  530.4 219.6 %all-reduce.7.cloned.1.call-start = ((), (), s32[]{:S(2)}) async-start(), calls=%async_computation.1 | async-start | bytes 196608 | tf_op jit(solution)/shard_map/psum | solution.py:34
Sparse Core Ops, SparseCore 0:
  23.9 107.4 all-gather.6
  134.0 70.2 all-gather.8
  206.4 70.5 all-gather.10
  530.5 136.5 all-reduce.4
  669.3 80.6 all-reduce.6
where the time goes:
time: 770 us; the launch traced here: 758 us
  waiting for transfers between devices  267 us (35%)
  other arithmetic  206 us (27%)
  local copies, waits for them, and re-layouts  157 us (20%)
  blocking collectives  85 us (11%)
  starting transfers between devices  21 us (3%)
  between operations  14.3 us (2%)
    psum x2, waiting for transfers between devices, one_axis_at_a_time(): return functools.reduce(lax.psum, axes, x)  133 us
    all_gather x3, waiting for transfers between devices, prefix_2(): everything = jax.tree.map(lambda part: lax.all_gather(part, axis), x)  115 us
    psum x2, blocking collectives, one_axis_at_a_time(): return functools.reduce(lax.psum, axes, x)  85 us
    reduce_sum x32, other arithmetic, retreat(): jnp.sum(tail * rate, axis=1)  39.3 us
    dynamic_slice x32, local copies, waits for them, and re-layouts, lap(): new = combine(before, jax.tree.map(lambda part: part[at], everything))  38.8 us
    add x32, other arithmetic, retreat(): values[position] * through_write + jnp.sum(tail * rate, axis=1)  32.8 us
    slice x16, local copies, waits for them, and re-layouts, advance(): weights[position][:, None] * write_rows[position][None, :]  29.3 us
    slice x16, local copies, waits for them, and re-layouts, retreat(): adjoint = read_rows[position][None, :] * outs[position][:, None] + back  28.9 us
  transfers between devices with their start and end apart: 10, of which 6 were waited for; matrix products, arithmetic and copies ran while one was open for 14% of the time, Pallas kernels for 0%

commit v1 on v0

v1 whole, which is shorter than its diff:
```python
import functools
import math

import jax
import jax.numpy as jnp
from jax import lax
from jax.experimental import pallas as pl
from jax.experimental.pallas import tpu as pltpu
from jax.sharding import PartitionSpec as P

HD = 96
WINDOW = 128
CHUNKS = 8
LANES = 128
BLOCK = 8
NEG = -1e30
BIG = 1e30
LOG2E = math.log2(math.e)
LN2 = math.log(2.0)
MESH = pl.DeviceIdType.MESH
F32 = jnp.float32
BF16 = jnp.bfloat16


def by_distance(count):
    return sorted(range(1, count), key=lambda d: -min(d, count - d))


def exchange(axis, count, me, source, landing, send_sem, recv_sem, slotted):
    copies = []
    for d in by_distance(count):
        peer = lax.rem(me + d, count)
        copy = pltpu.make_async_remote_copy(
            src_ref=source.at[peer] if slotted else source,
            dst_ref=landing.at[me],
            send_sem=send_sem.at[d],
            recv_sem=recv_sem.at[me],
            device_id={axis: peer},
            device_id_type=MESH,
        )
        copy.start()
        copies.append(copy)
    return copies


def arrivals(axis, count, me, source, landing, send_sem, recv_sem, slotted):
    for d in by_distance(count)[::-1]:
        peer = lax.rem(me + d, count)
        pltpu.make_async_remote_copy(
            src_ref=source.at[peer] if slotted else source,
            dst_ref=landing.at[peer],
            send_sem=send_sem.at[d],
            recv_sem=recv_sem.at[peer],
            device_id={axis: peer},
            device_id_type=MESH,
        ).wait_recv()


def shifted_rows(value, steps):
    return pltpu.roll(value, steps % CHUNKS, 0)


def prepare(sizes, x_ref, raw_ref, dy_ref, bias_ref, w_ref, r_ref, sc):
    groups, states, steps = sizes
    for n in range(states):
        sc["wb"][:, n] = jnp.broadcast_to(
            w_ref[:, n : n + 1], (steps * CHUNKS, LANES)
        ).reshape(steps, CHUNKS, LANES)
        sc["rb"][:, n] = jnp.broadcast_to(
            r_ref[:, n : n + 1], (steps * CHUNKS, LANES)
        ).reshape(steps, CHUNKS, LANES)

    def one(g, carry):
        lanes = pl.ds(pl.multiple_of(g * LANES, LANES), LANES)
        z = raw_ref[0, :, lanes].astype(F32) + bias_ref[g]
        small = jnp.exp(-jnp.abs(z))
        step = jnp.maximum(z, 0.0) + jnp.log(1.0 + small)
        sig = jnp.where(z >= 0, 1.0, small) / (1.0 + small)
        for at, value in enumerate(
            (step, sig, x_ref[0, :, lanes].astype(F32), dy_ref[0, :, lanes].astype(F32))
        ):
            sc["nat"][at] = value
            for i in range(steps):
                sc["items"][at, g, i] = sc["nat"].at[at][pl.ds(i, CHUNKS, stride=steps), :]
        return carry

    lax.fori_loop(0, groups, one, 0)


def summarize(sizes, rate_ref, sc):
    groups, states, steps = sizes
    chunk = lax.broadcasted_iota(jnp.int32, (CHUNKS, LANES), 0)

    def one(g, carry):
        total = sc["items"][0, g, 0]
        for i in range(1, steps):
            total = total + sc["items"][0, g, i]
        ahead, behind = ({1: total}, {1: total})
        for d in (1, 2, 4):
            ahead[2 * d] = ahead[d] + jnp.where(chunk >= d, shifted_rows(ahead[d], d), 0.0)
            behind[2 * d] = behind[d] + jnp.where(
                chunk < CHUNKS - d, shifted_rows(behind[d], -d), 0.0
            )
        sc["before"][g] = ahead[8] - total
        sc["after"][g] = behind[8] - total
        whole = ahead[8][CHUNKS - 1 : CHUNKS]
        ahead = {d: jnp.where(chunk >= d, ahead[d], BIG) for d in (1, 2, 4)}
        behind = {d: jnp.where(chunk < CHUNKS - d, behind[d], BIG) for d in (1, 2, 4)}

        for block in range(0, states, BLOCK):
            rate = [
                jnp.broadcast_to(rate_ref[g, n : n + 1, :], (CHUNKS, LANES))
                for n in range(block, block + BLOCK)
            ]

            def lap(i, state):
                ending, leading, through = state
                size = sc["items"][0, g, i]
                weight = size * sc["items"][2, g, i]
                out = sc["items"][3, g, i]
                new_e, new_l, new_t = ([], [], [])
                for k in range(BLOCK):
                    decay = jnp.exp2(rate[k] * size)
                    passed = through[k] * decay
                    new_e.append(decay * ending[k] + weight * sc["wb"][i, block + k])
                    new_l.append(leading[k] + passed * (out * sc["rb"][i, block + k]))
                    new_t.append(passed)
                return (tuple(new_e), tuple(new_l), tuple(new_t))

            zero = jnp.zeros((CHUNKS, LANES), F32)
            ending, leading, _ = lax.fori_loop(
                0,
                steps,
                lap,
                ((zero,) * BLOCK, (zero,) * BLOCK, (jnp.ones((CHUNKS, LANES), F32),) * BLOCK),
                unroll=4,
            )
            for k in range(BLOCK):
                n = block + k
                e, b = (ending[k], leading[k])
                for d in (1, 2, 4):
                    e = e + jnp.exp2(rate[k] * ahead[d]) * shifted_rows(e, d)
                    b = b + jnp.exp2(rate[k] * behind[d]) * shifted_rows(b, -d)
                sc["chunk_e"][g, n] = e
                sc["chunk_b"][g, n] = b
                sc["wide"][n, pl.ds(g, 1), :] = e[CHUNKS - 1 : CHUNKS]
                sc["wide"][n, pl.ds(16 + g, 1), :] = b[0:1]
                sc["wide"][n, pl.ds(32 + g, 1), :] = whole
        return carry

    sc["wide"][...] = jnp.zeros(sc["wide"].shape, F32)
    lax.fori_loop(0, groups, one, 0)
    sc["send1"][...] = sc["wide"][...].astype(BF16)


def starts(count, me, rate_rows_ref, sc):
    sc["recv1"][me] = sc["send1"][me]
    rate = rate_rows_ref[me]
    zero = jnp.zeros((16, LANES), F32)
    state, back = (zero, zero)
    for j in range(count):
        sc["send2"][j, 0:16] = state.astype(BF16)
        ending = sc["recv1"][j, 0:16].astype(F32)
        total = sc["recv1"][j, 32:48].astype(F32)
        state = jnp.exp2(rate * total) * state + ending
        k = count - 1 - j
        sc["send2"][k, 16:32] = back.astype(BF16)
        leading = sc["recv1"][k, 16:32].astype(F32)
        total = sc["recv1"][k, 32:48].astype(F32)
        back = jnp.exp2(rate * total) * back + leading
    sc["recv2"][me] = sc["send2"][me]


def finish(sizes, rate_ref, skip_ref, y_ref, xg_ref, rg_ref, sc):
    groups, states, steps = sizes
    chunk = lax.broadcasted_iota(jnp.int32, (CHUNKS, LANES), 0)
    sc["starts"][...] = sc["recv2"][...].astype(F32)
    sc["sums"][...] = jnp.zeros(sc["sums"].shape, F32)

    def one(g, carry):
        skip = skip_ref[g]
        lanes = pl.ds(pl.multiple_of(g * LANES, LANES), LANES)
        before, after = (sc["before"][g], sc["after"][g])
        for block in range(0, states, BLOCK):
            rate, state, back = ([], [], [])
            for n in range(block, block + BLOCK):
                r = jnp.broadcast_to(rate_ref[g, n : n + 1, :], (CHUNKS, LANES))
                rate.append(r)
                e = jnp.where(chunk >= 1, shifted_rows(sc["chunk_e"][g, n], 1), 0.0)
                b = jnp.where(chunk < CHUNKS - 1, shifted_rows(sc["chunk_b"][g, n], -1), 0.0)
                state.append(e + jnp.exp2(r * before) * sc["starts"][n, pl.ds(g, 1), :])
                back.append(b + jnp.exp2(r * after) * sc["starts"][n, pl.ds(16 + g, 1), :])

            def ahead(i, h):
                size = sc["items"][0, g, i]
                weight = size * sc["items"][2, g, i]
                if block == 0:
                    mixed = skip * sc["items"][2, g, i]
                else:
                    mixed = sc["mixed"][i]
                new = []
                for k in range(BLOCK):
                    moved = jnp.exp2(rate[k] * size) * h[k]
                    sc["moved"][i, k] = moved
                    value = moved + weight * sc["wb"][i, block + k]
                    mixed = mixed + value * sc["rb"][i, block + k]
                    new.append(value)
                sc["mixed"][i] = mixed
                return tuple(new)

            lax.fori_loop(0, steps, ahead, tuple(state), unroll=4)

            def retreat(lap, carry):
                back, total = carry
                i = steps - 1 - lap
                size = sc["items"][0, g, i]
                out = sc["items"][3, g, i]
                if block == 0:
                    written = jnp.zeros((CHUNKS, LANES), F32)
                    turned = jnp.zeros((CHUNKS, LANES), F32)
                else:
                    written = sc["written"][i]
                    turned = sc["turned"][i]
                new_b, new_t = ([], [])
                for k in range(BLOCK):
                    grown = rate[k] * size
                    adjoint = out * sc["rb"][i, block + k] + back[k]
                    written = written + adjoint * sc["wb"][i, block + k]
                    part = adjoint * sc["moved"][i, k] * grown
                    turned = turned + part
                    new_t.append(total[k] + part)
                    new_b.append(jnp.exp2(grown) * adjoint)
                sc["written"][i] = written
                sc["turned"][i] = turned
                return (tuple(new_b), tuple(new_t))

            zero = jnp.zeros((CHUNKS, LANES), F32)
            _, total = lax.fori_loop(
                0, steps, retreat, (tuple(back), (zero,) * BLOCK), unroll=4
            )
            for k in range(BLOCK):
                sc["sums"][block + k, pl.ds(g, 1), :] = LN2 * jnp.sum(
                    total[k], axis=0, keepdims=True
                )
        bias_sum = jnp.zeros((CHUNKS, LANES), F32)
        skip_sum = jnp.zeros((CHUNKS, LANES), F32)
        for i in range(steps):
            size, sig = (sc["items"][0, g, i], sc["items"][1, g, i])
            x, out = (sc["items"][2, g, i], sc["items"][3, g, i])
            written = sc["written"][i]
            raw = (x * written + LN2 * sc["turned"][i] / size) * sig
            bias_sum = bias_sum + raw
            skip_sum = skip_sum + out * x
            rows = pl.ds(i, CHUNKS, stride=steps)
            sc["nat"].at[0][rows, :] = sc["mixed"][i]
            sc["nat"].at[1][rows, :] = written * size + skip * out
            sc["nat"].at[2][rows, :] = raw
        y_ref[0, :, lanes] = sc["nat"][0].astype(BF16)
        xg_ref[0, :, lanes] = sc["nat"][1].astype(BF16)
        rg_ref[0, :, lanes] = sc["nat"][2].astype(BF16)
        sc["sums"][lax.div(g, 2), pl.ds(groups + lax.rem(g, 2), 1), :] = jnp.sum(
            bias_sum, axis=0, keepdims=True
        )
        h = g + groups
        sc["sums"][lax.div(h, 2), pl.ds(groups + lax.rem(h, 2), 1), :] = jnp.sum(
            skip_sum, axis=0, keepdims=True
        )
        return carry

    lax.fori_loop(0, groups, one, 0)
    sc["send3"][...] = sc["sums"][...].astype(BF16)


MIXER_SCRATCH = (
    "wb", "rb", "nat", "items", "before", "after", "chunk_e", "chunk_b", "wide", "send1", "recv1",
    "send2", "recv2", "starts", "sums", "moved", "mixed", "written", "turned", "send3", "recv3",
    "send4", "recv4", "send5", "recv5",
)


def mixer_kernel(sizes, seq, dp, *refs):
    (x_ref, raw_ref, dy_ref, bias_ref, skip_ref, rate_ref, rate_rows_ref, w_ref, r_ref) = refs[:9]
    y_ref, xg_ref, rg_ref, red_ref = refs[9:13]
    sc = dict(zip(MIXER_SCRATCH, refs[13:]))
    send_sem, recv_sem = refs[13 + len(MIXER_SCRATCH) :]
    me = lax.axis_index("seq")
    row = lax.axis_index("dp")

    barrier = pltpu.get_barrier_semaphore()
    for d in range(1, seq):
        pl.semaphore_signal(
            barrier, inc=1, device_id={"seq": lax.rem(me + d, seq)}, device_id_type=MESH
        )
    for d in range(1, dp):
        pl.semaphore_signal(
            barrier, inc=1, device_id={"dp": lax.rem(row + d, dp)}, device_id_type=MESH
        )
    prepare(sizes, x_ref, raw_ref, dy_ref, bias_ref, w_ref, r_ref, sc)
    summarize(sizes, rate_ref, sc)
    pl.semaphore_wait(barrier, seq + dp - 2)

    def run(stage, axis, count, at, source, landing, slotted):
        args = (axis, count, at, source, landing, send_sem.at[stage], recv_sem.at[stage], slotted)
        copies = exchange(*args)
        arrivals(*args)
        return copies

    copies = run(0, "seq", seq, me, sc["send1"], sc["recv1"], True)
    starts(seq, me, rate_rows_ref, sc)
    copies += run(1, "seq", seq, me, sc["send2"], sc["recv2"], True)
    finish(sizes, rate_ref, skip_ref, y_ref, xg_ref, rg_ref, sc)
    copies += run(2, "seq", seq, me, sc["send3"], sc["recv3"], True)
    sc["recv3"][me] = sc["send3"][me]
    part = jnp.sum(sc["recv3"][...].astype(F32), axis=0)
    sc["send4"][...] = part.astype(BF16)
    copies += run(3, "dp", dp, row, sc["send4"], sc["recv4"], False)
    sc["recv4"][row] = sc["send4"][...]
    sc["send5"][...] = jnp.sum(sc["recv4"][...].astype(F32), axis=0).astype(BF16)
    copies += run(4, "seq", seq, me, sc["send5"], sc["recv5"], False)
    sc["recv5"][me] = sc["send5"][...]
    red_ref[...] = sc["recv5"][...].astype(F32)
    for copy in copies:
        copy.wait_send()


def mixer(x, raw, dy, bias, decay_log, skip, write, read):
    seq, dp = (lax.axis_size("seq"), lax.axis_size("dp"))
    _, length, channels = x.shape
    states = decay_log.shape[1]
    groups, steps = (channels // LANES, length // CHUNKS)
    sizes = (groups, states, steps)
    rate = (-LOG2E * jnp.exp(decay_log)).reshape(groups, LANES, states)
    rate_gn = rate.transpose(0, 2, 1)
    rate_ng = jnp.pad(rate.transpose(2, 0, 1), ((0, 0), (0, 16 - groups), (0, 0)))

    def ordered(values):
        return (
            values[0].astype(F32).reshape(CHUNKS, steps, states).transpose(1, 0, 2)
        ).reshape(length, states)

    grid = (steps, states, CHUNKS, LANES)
    line = (steps, CHUNKS, LANES)
    vmem = {
        "wb": (grid, F32),
        "rb": (grid, F32),
        "nat": ((4, length, LANES), F32),
        "items": ((4, groups) + line, F32),
        "before": ((groups, CHUNKS, LANES), F32),
        "after": ((groups, CHUNKS, LANES), F32),
        "chunk_e": ((groups, states, CHUNKS, LANES), F32),
        "chunk_b": ((groups, states, CHUNKS, LANES), F32),
        "wide": ((states, 48, LANES), F32),
        "send1": ((states, 48, LANES), BF16),
        "recv1": ((seq, 48, LANES), BF16),
        "send2": ((seq, 32, LANES), BF16),
        "recv2": ((states, 32, LANES), BF16),
        "starts": ((states, 32, LANES), F32),
        "sums": ((states, 16, LANES), F32),
        "moved": ((steps, BLOCK, CHUNKS, LANES), F32),
        "mixed": (line, F32),
        "written": (line, F32),
        "turned": (line, F32),
        "send3": ((states, 16, LANES), BF16),
        "recv3": ((seq, 16, LANES), BF16),
        "send4": ((16, LANES), BF16),
        "recv4": ((dp, 16, LANES), BF16),
        "send5": ((16, LANES), BF16),
        "recv5": ((states, 16, LANES), BF16),
    }
    inside = pl.BlockSpec(memory_space=pltpu.VMEM)
    y, xg, rg, red = pl.pallas_call(
        functools.partial(mixer_kernel, sizes, seq, dp),
        out_shape=(
            jax.ShapeDtypeStruct(x.shape, BF16),
            jax.ShapeDtypeStruct(x.shape, BF16),
            jax.ShapeDtypeStruct(x.shape, BF16),
            jax.ShapeDtypeStruct((states, 16, LANES), F32),
        ),
        in_specs=[inside] * 9,
        out_specs=(inside,) * 4,
        scratch_shapes=[pltpu.VMEM(*vmem[name]) for name in MIXER_SCRATCH]
        + [pltpu.SemaphoreType.DMA((5, seq))] * 2,
        compiler_params=pltpu.CompilerParams(
            collective_id=0, has_side_effects=True, vmem_limit_bytes=48 << 20
        ),
        cost_estimate=pl.CostEstimate(
            flops=40 * length * channels * states, bytes_accessed=16 * length * channels,
            transcendentals=4 * length * channels * states,
        ),
        name="mixer",
    )(
        x,
        raw,
        dy,
        bias.reshape(groups, 1, LANES),
        skip.reshape(groups, 1, LANES),
        rate_gn,
        rate_ng,
        ordered(write),
        ordered(read),
    )
    scale = 1.0 / math.sqrt(length * seq * dp)
    decay = red[:, :groups].reshape(states, channels).T * scale
    rows = red[:, groups : groups + 2].reshape(2 * states, LANES) * scale
    return (
        y,
        xg,
        rg,
        decay,
        rows[groups : 2 * groups].reshape(channels),
        rows[:groups].reshape(channels),
    )


def window_kernel(
    q_ref, k_ref, v_ref, do_ref, kb_ref, vb_ref, doc_col_ref, doc_row_ref,
    o_ref, dq_ref, dk_ref, dv_ref, dkb_ref, dvb_ref,
):
    length, width = q_ref.shape[1:]
    scale = 1.0 / math.sqrt(HD)
    query = lax.broadcasted_iota(jnp.int32, (length, 2 * length), 0)
    key = lax.broadcasted_iota(jnp.int32, (length, 2 * length), 1)
    offset = query + length - key
    allowed = (offset >= 0) & (offset < WINDOW) & (doc_row_ref[...] == doc_col_ref[...])
    for head in range(width // HD):
        at = slice(head * HD, (head + 1) * HD)
        q, do = (q_ref[0, :, at], do_ref[0, :, at])
        k = jnp.concatenate([kb_ref[0, :, at], k_ref[0, :, at]], axis=0)
        v = jnp.concatenate([vb_ref[0, :, at], v_ref[0, :, at]], axis=0)
        over_lanes = (((1,), (1,)), ((), ()))
        over_rows = (((0,), (0,)), ((), ()))
        plain = (((1,), (0,)), ((), ()))
        scores = lax.dot_general(q, k, over_lanes, preferred_element_type=F32) * scale
        scores = jnp.where(allowed, scores, NEG)
        top = jnp.max(scores, axis=1, keepdims=True)
        raised = jnp.exp(scores - top)
        probs = raised / jnp.sum(raised, axis=1, keepdims=True)
        low = probs.astype(BF16)
        out = lax.dot_general(low, v, plain, preferred_element_type=F32).astype(BF16)
        row_term = jnp.sum(do.astype(F32) * out.astype(F32), axis=1, keepdims=True)
        value_score = lax.dot_general(do, v, over_lanes, preferred_element_type=F32)
        grad = (probs * (value_score - row_term)).astype(BF16)
        o_ref[0, :, at] = out
        dq_ref[0, :, at] = (
            lax.dot_general(grad, k, plain, preferred_element_type=F32) * scale
        ).astype(BF16)
        dk = lax.dot_general(grad, q, over_rows, preferred_element_type=F32) * scale
        dv = lax.dot_general(low, do, over_rows, preferred_element_type=F32)
        dkb_ref[0, :, at] = dk[:length].astype(BF16)
        dvb_ref[0, :, at] = dv[:length].astype(BF16)
        dk_ref[0, :, at] = dk[length:]
        dv_ref[0, :, at] = dv[length:]


def shifted(value, steps):
    count = lax.axis_size("seq")
    leading, last = (max(0, -steps), min(count, count - steps))
    return lax.ppermute(value, "seq", [(source, source + steps) for source in range(leading, last)])


def window(query, key, value, out_grad, docs):
    length = query.shape[1]
    doc_now = docs + 1
    key_before, value_before = (shifted(key, 1), shifted(value, 1))
    doc_before = shifted(doc_now, 1)
    doc_row = jnp.concatenate([doc_before, doc_now], axis=1)
    inside = pl.BlockSpec(memory_space=pltpu.VMEM)
    wide = jax.ShapeDtypeStruct(query.shape, F32)
    low = jax.ShapeDtypeStruct(query.shape, BF16)
    out, dq, dk, dv, dkb, dvb = pl.pallas_call(
        window_kernel,
        out_shape=(low, low, wide, wide, low, low),
        in_specs=[inside] * 8,
        out_specs=(inside,) * 6,
        compiler_params=pltpu.CompilerParams(vmem_limit_bytes=48 << 20),
        cost_estimate=pl.CostEstimate(
            flops=20 * length * length * query.shape[2],
            bytes_accessed=24 * length * query.shape[2],
            transcendentals=0,
        ),
        name="window",
    )(query, key, value, out_grad, key_before, value_before, doc_now.reshape(length, 1), doc_row)
    dk = dk + shifted(dkb, -1).astype(F32)
    dv = dv + shifted(dvb, -1).astype(F32)
    return (out, dq, dk.astype(BF16), dv.astype(BF16))


def body(
    mixer_in,
    delta_raw,
    delta_bias,
    decay_log,
    skip_gain,
    state_write,
    state_read,
    mixer_grad,
    attn_query,
    attn_key,
    attn_value,
    attn_grad,
    document_id,
):
    scanned = mixer(
        mixer_in, delta_raw, mixer_grad, delta_bias, decay_log, skip_gain, state_write, state_read
    )
    attended = window(attn_query, attn_key, attn_value, attn_grad, document_id)
    return scanned + attended


def solution(mesh):
    spread = P(("member", "dp"), "seq", "mp")
    shared = P(("member", "dp"), "seq", None)
    one = P(("member", "mp"))
    two = P(("member", "mp"), None)
    return jax.shard_map(
        body,
        mesh=mesh,
        in_specs=(
            spread,
            spread,
            one,
            two,
            one,
            shared,
            shared,
            spread,
            spread,
            spread,
            spread,
            spread,
            P(("member", "dp"), "seq"),
        ),
        out_specs=(spread, spread, spread, two, one, one, spread, spread, spread, spread),
        check_vma=False,
    )
```

time: 770 us -> 136 us (0.18); the launches traced: 758 us -> 136 us
  waiting for transfers between devices: 267 us -> 6.22 us
  other arithmetic: 206 us -> 3.02 us
  local copies, waits for them, and re-layouts: 157 us -> 6.85 us
  Pallas kernels: 0 us -> 98.1 us
  blocking collectives: 85 us -> 0 us
  between operations: 14.3 us -> 0.89 us
    psum x2 -> x0, waiting for transfers between devices: 133 us -> none  [one_axis_at_a_time(): return functools.reduce(lax.psum, axes, x)]
    all_gather x3 -> x0, waiting for transfers between devices: 115 us -> none  [prefix_2(): everything = jax.tree.map(lambda part: lax.all_gather(part, axis), x)]
    pallas_call x0 -> x2, Pallas kernels: none -> 98.1 us  [the longest x1 91.3 us: mixer(): pl.pallas_call(functools.partial(mixer_kernel, sizes, seq, dp), out_shape...]
    psum x2 -> x0, blocking collectives: 85 us -> none  [one_axis_at_a_time(): return functools.reduce(lax.psum, axes, x)]
    add x66 -> x1, other arithmetic: 84.4 us -> 0.66 us  [window(): doc_now = docs + 1]
    reduce_sum x84 -> x0, other arithmetic: 75.4 us -> none  [the longest x32 39.3 us: retreat(): jnp.sum(tail * rate, axis=1)]
    slice x40 -> x1, local copies, waits for them, and re-layouts: 73 us -> 0.01 us  [mixer(): rows[:groups].reshape(channels)]
    dynamic_slice x64 -> x0, local copies, waits for them, and re-layouts: 39 us -> none  [the longest x32 38.8 us: lap(): new = combine(before, jax.tree.map(lambda part: part[at], everything))]
  transfers between devices with their start and end apart: 10 -> 5, of which waited for: 6 -> 2; matrix products, arithmetic and copies ran while one was open for 14% -> 3% of each run, Pallas kernels for 0% -> 67%
where the time goes in v1:
time: 136 us
  Pallas kernels  98.1 us (72%)
  starting transfers between devices  20.7 us (15%)
  local copies, waits for them, and re-layouts  6.85 us (5%)
  waiting for transfers between devices  6.22 us (5%)
  other arithmetic  3.02 us (2%)
    pallas_call x1, Pallas kernels, mixer(): pl.pallas_call(functools.partial(mixer_kernel, sizes, seq, dp), out_shape...  91.3 us
    ppermute x5, starting transfers between devices, shifted(): lax.ppermute(value, 'seq', [(source, source + steps) for source in range(...  20.7 us
    pallas_call x1, Pallas kernels, window(): pl.pallas_call(window_kernel, out_shape=(low, low, wide, wide, low, low),...  6.74 us
    ppermute x5, waiting for transfers between devices, shifted(): lax.ppermute(value, 'seq', [(source, source + steps) for source in range(...  6.22 us
    unnamed x26, local copies, waits for them, and re-layouts  5.1 us
  transfers between devices with their start and end apart: 5, of which 2 were waited for; matrix products, arithmetic and copies ran while one was open for 3% of the time, Pallas kernels for 67%

profile of v1, /device:TPU:80, one launch (start us, length us, event | category | flops | bytes accessed | tf_op | source)
XLA Modules:
  0.0 135.7 jit_solution(18306684793895284625)
XLA Ops:
  0.6 0.7 broadcast_add_fusion
  1.3 6.0 %collective-permute-start.2 = (s32[1,128]{1,0:T(1,128)S(1)}, s32[1,128]{1,0:T(1,128)S(1)}, u32[]{:S(2)}, u32[]{:S(2)}) collective-permute-start(s32[1,128]{1,0:T(1,128)S(1)} %get-tuple-element.34), channel_id=1, source_target_pairs={{0,16},{16,32},{32,48},{48,64},{64,80},{80,96},{96,112},{112,128},... | collective-permute-start | bytes 1544 | tf_op jit(solution)/shard_map/ppermute | solution.py:458
  7.3 6.0 %collective-permute-start = (bf16[1,128,768]{2,1,0:T(8,128)(2,1)}, bf16[1,128,768]{2,1,0:T(8,128)(2,1)S(1)}, u32[]{:S(2)}, u32[]{:S(2)}) collective-permute-start(bf16[1,128,768]{2,1,0:T(8,128)(2,1)} %k_ref.1), channel_id=1, source_target_pairs={{0,16},{16,32},{32,48},{48,64},{64,80},{80,96},{96,112},{112,128},... | collective-permute-start | bytes 589832 | tf_op jit(solution)/shard_map/ppermute | solution.py:458
  13.4 6.0 %collective-permute-start.1 = (bf16[1,128,768]{2,1,0:T(8,128)(2,1)}, bf16[1,128,768]{2,1,0:T(8,128)(2,1)S(1)}, u32[]{:S(2)}, u32[]{:S(2)}) collective-permute-start(bf16[1,128,768]{2,1,0:T(8,128)(2,1)} %v_ref.1), channel_id=1, source_target_pairs={{0,16},{16,32},{32,48},{48,64},{64,80},{80,96},{96,112},{112,128},... | collective-permute-start | bytes 589832 | tf_op jit(solution)/shard_map/ppermute | solution.py:458
  19.4 0.9 exponential_multiply_fusion
  20.3 0.0 copy-start.9
  20.3 0.0 copy-start.10
  20.4 0.0 copy-start.7
  20.4 0.0 copy-start.8
  20.4 0.0 copy-start.5
  20.4 0.6 copy-done.9
  21.0 0.0 copy-start.4
  21.0 0.1 reshape.83
  21.1 0.1 copy.28
  21.2 0.0 copy-done.10
  21.2 0.1 reshape.85
  21.3 0.1 copy.29
  21.4 0.0 copy-done.7
  21.4 0.0 copy-done.8
  21.5 0.0 copy-done.5
  21.5 0.6 copy-done.4
  22.0 0.0 copy-start.6
  22.1 1.0 copy-done.6
  23.0 0.0 copy-start
  23.0 0.0 copy-start.1
  23.0 0.0 copy-start.2
  23.1 91.3 %mixer.1 = (bf16[1,128,1536]{2,1,0:T(8,128)(2,1)S(1)}, bf16[1,128,1536]{2,1,0:T(8,128)(2,1)S(1)}, bf16[1,128,1536]{2,1,0:T(8,128)(2,1)S(1)}, f32[16,16,128]{2,1,0:T(8,128)S(1)}) custom-call(bf16[1,128,1536]{2,1,0:T(8,128)(2,1)S(1)} %copy-done.4, bf16[1,128,1536]{2,1,0:T(8,128)(2,1)S(1)} %copy-done.5, bf16[1,128,1536]{2,1,0:T(8,128)(2,1)S(1)} %copy-done.6, ...), custom_call_target="tpu_custom_call" | custom-call | flops 125829120 | bytes 3145728 | tf_op jit(solution)/shard_map/mixer/pallas_call | solution.py:371
  114.4 0.1 copy.30.doc_col_ref
  114.5 0.6 reshape.73
  115.2 0.6 reshape.74
  115.8 0.0 collective-permute-done.2
  115.8 0.0 collective-permute-done.kb_ref
  115.8 0.0 collective-permute-done.1.vb_ref
  115.8 0.0 copy-done
  115.8 0.0 copy-done.1
  115.8 0.0 copy-done.2
  115.8 0.0 copy-done.3
  115.8 6.7 %window.1 = (bf16[1,128,768]{2,1,0:T(8,128)(2,1)}, bf16[1,128,768]{2,1,0:T(8,128)(2,1)}, f32[1,128,768]{2,1,0:T(8,128)S(1)}, f32[1,128,768]{2,1,0:T(8,128)S(1)},...) custom-call(bf16[1,128,768]{2,1,0:T(8,128)(2,1)S(1)} %copy-done, bf16[1,128,768]{2,1,0:T(8,128)(2,1)S(1)} %copy-done.1, ...), custom_call_target="tpu_custom_call" | custom-call | flops 251658240 | bytes 2359296 | tf_op jit(solution)/shard_map/window/pallas_call | solution.py:470
  122.6 1.3 collective-permute-start.4
  123.9 0.7 copy.39
  124.6 1.3 collective-permute-start.3
  125.9 4.3 %collective-permute-done.4 = bf16[1,128,768]{2,1,0:T(8,128)(2,1)S(1)} collective-permute-done((bf16[1,128,768]{2,1,0:T(8,128)(2,1)S(1)}, bf16[1,128,768]{2,1,0:T(8,128)(2,1)S(1)}, u32[]{:S(2)}, u32[]{:S(2)}) %collective-permute-start.4) | collective-permute-done | bytes 196640 | tf_op jit(solution)/shard_map/ppermute | solution.py:458
  130.1 0.7 add_convert_fusion
  130.9 1.9 %collective-permute-done.3 = bf16[1,128,768]{2,1,0:T(8,128)(2,1)S(1)} collective-permute-done((bf16[1,128,768]{2,1,0:T(8,128)(2,1)S(1)}, bf16[1,128,768]{2,1,0:T(8,128)(2,1)S(1)}, u32[]{:S(2)}, u32[]{:S(2)}) %collective-permute-start.3) | collective-permute-done | bytes 196640 | tf_op jit(solution)/shard_map/ppermute | solution.py:458
  132.8 0.7 add_convert_fusion.1
  133.5 0.7 copy.44
  134.2 0.7 copy.45
  135.0 0.7 copy.46
  (10 shorter events, 0.1 us)
Async XLA Ops:
  1.3 114.5 %collective-permute-start.2 = (s32[1,128]{1,0:T(1,128)S(1)}, s32[1,128]{1,0:T(1,128)S(1)}, u32[]{:S(2)}, u32[]{:S(2)}) collective-permute-start(s32[1,128]{1,0:T(1,128)S(1)} %get-tuple-element.34), channel_id=1, source_target_pairs={{0,16},{16,32},{32,48},{48,64},{64,80},{80,96},{96,112},{112,128},... | collective-permute-start | bytes 1544 | tf_op jit(solution)/shard_map/ppermute | solution.py:458
  7.3 108.4 %collective-permute-start = (bf16[1,128,768]{2,1,0:T(8,128)(2,1)}, bf16[1,128,768]{2,1,0:T(8,128)(2,1)S(1)}, u32[]{:S(2)}, u32[]{:S(2)}) collective-permute-start(bf16[1,128,768]{2,1,0:T(8,128)(2,1)} %k_ref.1), channel_id=1, source_target_pairs={{0,16},{16,32},{32,48},{48,64},{64,80},{80,96},{96,112},{112,128},... | collective-permute-start | bytes 589832 | tf_op jit(solution)/shard_map/ppermute | solution.py:458
  13.4 102.4 %collective-permute-start.1 = (bf16[1,128,768]{2,1,0:T(8,128)(2,1)}, bf16[1,128,768]{2,1,0:T(8,128)(2,1)S(1)}, u32[]{:S(2)}, u32[]{:S(2)}) collective-permute-start(bf16[1,128,768]{2,1,0:T(8,128)(2,1)} %v_ref.1), channel_id=1, source_target_pairs={{0,16},{16,32},{32,48},{48,64},{64,80},{80,96},{96,112},{112,128},... | collective-permute-start | bytes 589832 | tf_op jit(solution)/shard_map/ppermute | solution.py:458
  20.3 0.7 copy-start.9
  20.3 0.9 copy-start.10
  20.4 1.0 copy-start.7
  20.4 1.0 copy-start.8
  20.4 1.1 copy-start.5
  21.0 1.0 copy-start.4
  22.0 1.0 copy-start.6
  23.0 92.7 %copy-start = (bf16[1,128,768]{2,1,0:T(8,128)(2,1)S(1)}, bf16[1,128,768]{2,1,0:T(8,128)(2,1)}, u32[]{:S(2)}) copy-start(bf16[1,128,768]{2,1,0:T(8,128)(2,1)} %q_ref.1) | copy-start | bytes 589828
  23.0 92.7 %copy-start.1 = (bf16[1,128,768]{2,1,0:T(8,128)(2,1)S(1)}, bf16[1,128,768]{2,1,0:T(8,128)(2,1)}, u32[]{:S(2)}) copy-start(bf16[1,128,768]{2,1,0:T(8,128)(2,1)} %k_ref.1) | copy-start | bytes 589828
  23.0 92.8 %copy-start.2 = (bf16[1,128,768]{2,1,0:T(8,128)(2,1)S(1)}, bf16[1,128,768]{2,1,0:T(8,128)(2,1)}, u32[]{:S(2)}) copy-start(bf16[1,128,768]{2,1,0:T(8,128)(2,1)} %v_ref.1) | copy-start | bytes 589828
  23.1 92.8 %copy-start.3 = (bf16[1,128,768]{2,1,0:T(8,128)(2,1)S(1)}, bf16[1,128,768]{2,1,0:T(8,128)(2,1)}, u32[]{:S(2)}) copy-start(bf16[1,128,768]{2,1,0:T(8,128)(2,1)} %do_ref.1) | copy-start | bytes 589828
  122.6 7.6 %collective-permute-start.4 = (bf16[1,128,768]{2,1,0:T(8,128)(2,1)S(1)}, bf16[1,128,768]{2,1,0:T(8,128)(2,1)S(1)}, u32[]{:S(2)}, u32[]{:S(2)}) collective-permute-start(bf16[1,128,768]{2,1,0:T(8,128)(2,1)S(1)} %get-tuple-element.29), channel_id=1, source_target_pairs={{16,0},{32,16},{48,32},{64,48},{80,64},{96,80},{112,96},{128,112},... | collective-permute-start | bytes 589832 | tf_op jit(solution)/shard_map/ppermute | solution.py:458
  124.6 8.2 %collective-permute-start.3 = (bf16[1,128,768]{2,1,0:T(8,128)(2,1)S(1)}, bf16[1,128,768]{2,1,0:T(8,128)(2,1)S(1)}, u32[]{:S(2)}, u32[]{:S(2)}) collective-permute-start(bf16[1,128,768]{2,1,0:T(8,128)(2,1)S(1)} %get-tuple-element.27), channel_id=1, source_target_pairs={{16,0},{32,16},{48,32},{64,48},{80,64},{96,80},{112,96},{128,112},... | collective-permute-start | bytes 589832 | tf_op jit(solution)/shard_map/ppermute | solution.py:458

commit v2 on v1

--- a/solution.py
+++ b/solution.py
@@ -60,24 +60,29 @@
     return pltpu.roll(value, steps % CHUNKS, 0)
 
 
-def prepare(sizes, x_ref, raw_ref, dy_ref, bias_ref, w_ref, r_ref, sc):
+def prepare(sizes, me, bias_ref, decay_ref, write_ref, read_ref, sc):
     groups, states, steps = sizes
-    for n in range(states):
-        sc["wb"][:, n] = jnp.broadcast_to(
-            w_ref[:, n : n + 1], (steps * CHUNKS, LANES)
-        ).reshape(steps, CHUNKS, LANES)
-        sc["rb"][:, n] = jnp.broadcast_to(
-            r_ref[:, n : n + 1], (steps * CHUNKS, LANES)
-        ).reshape(steps, CHUNKS, LANES)
+    rate = -LOG2E * jnp.exp(decay_ref[...])
+    for g in range(groups):
+        sc["rate"][g] = rate[:, g * LANES : (g + 1) * LANES]
+    sc["mine"][...] = jnp.zeros(sc["mine"].shape, F32)
+    for g in range(groups):
+        sc["mine"][g : g + 1] = sc["rate"][g, pl.ds(me, 1), :]
+    for source, name in ((write_ref, "wb"), (read_ref, "rb")):
+        sc["nat"][0, :, 0:states] = source[0].astype(F32).T
+        for i in range(steps):
+            rows = sc["nat"].at[0][pl.ds(i, CHUNKS, stride=steps), :]
+            for n in range(states):
+                sc[name][i, n] = jnp.broadcast_to(rows[:, n : n + 1], (CHUNKS, LANES))
 
     def one(g, carry):
         lanes = pl.ds(pl.multiple_of(g * LANES, LANES), LANES)
-        z = raw_ref[0, :, lanes].astype(F32) + bias_ref[g]
+        z = sc["raw"][:, lanes].astype(F32) + bias_ref[:, lanes]
         small = jnp.exp(-jnp.abs(z))
         step = jnp.maximum(z, 0.0) + jnp.log(1.0 + small)
         sig = jnp.where(z >= 0, 1.0, small) / (1.0 + small)
         for at, value in enumerate(
-            (step, sig, x_ref[0, :, lanes].astype(F32), dy_ref[0, :, lanes].astype(F32))
+            (step, sig, sc["x"][:, lanes].astype(F32), sc["dy"][:, lanes].astype(F32))
         ):
             sc["nat"][at] = value
             for i in range(steps):
@@ -87,7 +92,7 @@
     lax.fori_loop(0, groups, one, 0)
 
 
-def summarize(sizes, rate_ref, sc):
+def summarize(sizes, sc):
     groups, states, steps = sizes
     chunk = lax.broadcasted_iota(jnp.int32, (CHUNKS, LANES), 0)
 
@@ -109,7 +114,7 @@
 
         for block in range(0, states, BLOCK):
             rate = [
-                jnp.broadcast_to(rate_ref[g, n : n + 1, :], (CHUNKS, LANES))
+                jnp.broadcast_to(sc["rate"][g, n : n + 1, :], (CHUNKS, LANES))
                 for n in range(block, block + BLOCK)
             ]
 
@@ -153,9 +158,9 @@
     sc["send1"][...] = sc["wide"][...].astype(BF16)
 
 
-def starts(count, me, rate_rows_ref, sc):
+def starts(count, me, sc):
     sc["recv1"][me] = sc["send1"][me]
-    rate = rate_rows_ref[me]
+    rate = sc["mine"][...]
     zero = jnp.zeros((16, LANES), F32)
     state, back = (zero, zero)
     for j in range(count):
@@ -171,20 +176,20 @@
     sc["recv2"][me] = sc["send2"][me]
 
 
-def finish(sizes, rate_ref, skip_ref, y_ref, xg_ref, rg_ref, sc):
+def finish(sizes, skip_ref, y_ref, xg_ref, rg_ref, sc):
     groups, states, steps = sizes
     chunk = lax.broadcasted_iota(jnp.int32, (CHUNKS, LANES), 0)
     sc["starts"][...] = sc["recv2"][...].astype(F32)
     sc["sums"][...] = jnp.zeros(sc["sums"].shape, F32)
 
     def one(g, carry):
-        skip = skip_ref[g]
         lanes = pl.ds(pl.multiple_of(g * LANES, LANES), LANES)
+        skip = skip_ref[:, lanes]
         before, after = (sc["before"][g], sc["after"][g])
         for block in range(0, states, BLOCK):
             rate, state, back = ([], [], [])
             for n in range(block, block + BLOCK):
-                r = jnp.broadcast_to(rate_ref[g, n : n + 1, :], (CHUNKS, LANES))
+                r = jnp.broadcast_to(sc["rate"][g, n : n + 1, :], (CHUNKS, LANES))
                 rate.append(r)
                 e = jnp.where(chunk >= 1, shifted_rows(sc["chunk_e"][g, n], 1), 0.0)
                 b = jnp.where(chunk < CHUNKS - 1, shifted_rows(sc["chunk_b"][g, n], -1), 0.0)
@@ -271,76 +276,75 @@
     sc["send3"][...] = sc["sums"][...].astype(BF16)
 
 
-MIXER_SCRATCH = (
-    "wb", "rb", "nat", "items", "before", "after", "chunk_e", "chunk_b", "wide", "send1", "recv1",
-    "send2", "recv2", "starts", "sums", "moved", "mixed", "written", "turned", "send3", "recv3",
-    "send4", "recv4", "send5", "recv5",
-)
-
-
-def mixer_kernel(sizes, seq, dp, *refs):
-    (x_ref, raw_ref, dy_ref, bias_ref, skip_ref, rate_ref, rate_rows_ref, w_ref, r_ref) = refs[:9]
-    y_ref, xg_ref, rg_ref, red_ref = refs[9:13]
-    sc = dict(zip(MIXER_SCRATCH, refs[13:]))
-    send_sem, recv_sem = refs[13 + len(MIXER_SCRATCH) :]
-    me = lax.axis_index("seq")
-    row = lax.axis_index("dp")
-
-    barrier = pltpu.get_barrier_semaphore()
-    for d in range(1, seq):
-        pl.semaphore_signal(
-            barrier, inc=1, device_id={"seq": lax.rem(me + d, seq)}, device_id_type=MESH
-        )
-    for d in range(1, dp):
-        pl.semaphore_signal(
-            barrier, inc=1, device_id={"dp": lax.rem(row + d, dp)}, device_id_type=MESH
-        )
-    prepare(sizes, x_ref, raw_ref, dy_ref, bias_ref, w_ref, r_ref, sc)
-    summarize(sizes, rate_ref, sc)
-    pl.semaphore_wait(barrier, seq + dp - 2)
-
-    def run(stage, axis, count, at, source, landing, slotted):
-        args = (axis, count, at, source, landing, send_sem.at[stage], recv_sem.at[stage], slotted)
-        copies = exchange(*args)
-        arrivals(*args)
-        return copies
-
-    copies = run(0, "seq", seq, me, sc["send1"], sc["recv1"], True)
-    starts(seq, me, rate_rows_ref, sc)
-    copies += run(1, "seq", seq, me, sc["send2"], sc["recv2"], True)
-    finish(sizes, rate_ref, skip_ref, y_ref, xg_ref, rg_ref, sc)
-    copies += run(2, "seq", seq, me, sc["send3"], sc["recv3"], True)
-    sc["recv3"][me] = sc["send3"][me]
-    part = jnp.sum(sc["recv3"][...].astype(F32), axis=0)
-    sc["send4"][...] = part.astype(BF16)
-    copies += run(3, "dp", dp, row, sc["send4"], sc["recv4"], False)
-    sc["recv4"][row] = sc["send4"][...]
-    sc["send5"][...] = jnp.sum(sc["recv4"][...].astype(F32), axis=0).astype(BF16)
-    copies += run(4, "seq", seq, me, sc["send5"], sc["recv5"], False)
-    sc["recv5"][me] = sc["send5"][...]
-    red_ref[...] = sc["recv5"][...].astype(F32)
-    for copy in copies:
-        copy.wait_send()
-
-
-def mixer(x, raw, dy, bias, decay_log, skip, write, read):
-    seq, dp = (lax.axis_size("seq"), lax.axis_size("dp"))
-    _, length, channels = x.shape
-    states = decay_log.shape[1]
-    groups, steps = (channels // LANES, length // CHUNKS)
-    sizes = (groups, states, steps)
-    rate = (-LOG2E * jnp.exp(decay_log)).reshape(groups, LANES, states)
-    rate_gn = rate.transpose(0, 2, 1)
-    rate_ng = jnp.pad(rate.transpose(2, 0, 1), ((0, 0), (0, 16 - groups), (0, 0)))
-
-    def ordered(values):
-        return (
-            values[0].astype(F32).reshape(CHUNKS, steps, states).transpose(1, 0, 2)
-        ).reshape(length, states)
-
+def window(first, o_ref, dq_ref, doc_ref, sc):
+    length, width = sc["q"].shape
+    scale = 1.0 / math.sqrt(HD)
+    docs = doc_ref[...]
+    before = jnp.where(first, -1, sc["doc_in"][...])
+    own = jnp.broadcast_to(docs.astype(F32), (length, length)).T
+    own = jnp.concatenate([own, own], axis=1)
+    seen = jnp.concatenate([before, docs], axis=1).astype(F32)
+    query = lax.broadcasted_iota(jnp.int32, (length, 2 * length), 0)
+    key = lax.broadcasted_iota(jnp.int32, (length, 2 * length), 1)
+    offset = query + length - key
+    allowed = (offset >= 0) & (offset < WINDOW) & (own == seen)
+    over_lanes = (((1,), (1,)), ((), ()))
+    over_rows = (((0,), (0,)), ((), ()))
+    plain = (((1,), (0,)), ((), ()))
+    for head in range(width // HD):
+        at = slice(head * HD, (head + 1) * HD)
+        q, do = (sc["q"][:, at], sc["do"][:, at])
+        k = jnp.concatenate([sc["k_in"][:, at], sc["k"][:, at]], axis=0)
+        v = jnp.concatenate([sc["v_in"][:, at], sc["v"][:, at]], axis=0)
+        scores = lax.dot_general(q, k, over_lanes, preferred_element_type=F32) * scale
+        scores = jnp.where(allowed, scores, NEG)
+        top = jnp.max(scores, axis=1, keepdims=True)
+        raised = jnp.exp(scores - top)
+        probs = raised / jnp.sum(raised, axis=1, keepdims=True)
+        low = probs.astype(BF16)
+        out = lax.dot_general(low, v, plain, preferred_element_type=F32).astype(BF16)
+        row_term = jnp.sum(do.astype(F32) * out.astype(F32), axis=1, keepdims=True)
+        value_score = lax.dot_general(do, v, over_lanes, preferred_element_type=F32)
+        grad = (probs * (value_score - row_term)).astype(BF16)
+        o_ref[0, :, at] = out
+        dq_ref[0, :, at] = (
+            lax.dot_general(grad, k, plain, preferred_element_type=F32) * scale
+        ).astype(BF16)
+        dk = lax.dot_general(grad, q, over_rows, preferred_element_type=F32) * scale
+        dv = lax.dot_general(low, do, over_rows, preferred_element_type=F32)
+        sc["dk_out"][:, at] = dk[:length].astype(BF16)
+        sc["dv_out"][:, at] = dv[:length].astype(BF16)
+        sc["dk"][:, at] = dk[length:]
+        sc["dv"][:, at] = dv[length:]
+
+
+SEMAPHORES = ("load", "send", "recv", "halo_send", "halo_recv")
+
+
+def scratch_shapes(sizes, length, width, seq, dp):
+    groups, states, steps = sizes
+    channels = groups * LANES
     grid = (steps, states, CHUNKS, LANES)
     line = (steps, CHUNKS, LANES)
-    vmem = {
+    return {
+        "x": ((length, channels), BF16),
+        "raw": ((length, channels), BF16),
+        "dy": ((length, channels), BF16),
+        "q": ((length, width), BF16),
+        "k": ((length, width), BF16),
+        "v": ((length, width), BF16),
+        "do": ((length, width), BF16),
+        "k_in": ((length, width), BF16),
+        "v_in": ((length, width), BF16),
+        "doc_in": ((1, length), jnp.int32),
+        "dk": ((length, width), F32),
+        "dv": ((length, width), F32),
+        "dk_out": ((length, width), BF16),
+        "dv_out": ((length, width), BF16),
+        "dk_in": ((length, width), BF16),
+        "dv_in": ((length, width), BF16),
+        "rate": ((groups, states, LANES), F32),
+        "mine": ((16, LANES), F32),
         "wb": (grid, F32),
         "rb": (grid, F32),
         "nat": ((4, length, LANES), F32),
@@ -367,122 +371,117 @@
         "send5": ((16, LANES), BF16),
         "recv5": ((states, 16, LANES), BF16),
     }
-    inside = pl.BlockSpec(memory_space=pltpu.VMEM)
-    y, xg, rg, red = pl.pallas_call(
-        functools.partial(mixer_kernel, sizes, seq, dp),
-        out_shape=(
-            jax.ShapeDtypeStruct(x.shape, BF16),
-            jax.ShapeDtypeStruct(x.shape, BF16),
-            jax.ShapeDtypeStruct(x.shape, BF16),
-            jax.ShapeDtypeStruct((states, 16, LANES), F32),
-        ),
-        in_specs=[inside] * 9,
-        out_specs=(inside,) * 4,
-        scratch_shapes=[pltpu.VMEM(*vmem[name]) for name in MIXER_SCRATCH]
-        + [pltpu.SemaphoreType.DMA((5, seq))] * 2,
-        compiler_params=pltpu.CompilerParams(
-            collective_id=0, has_side_effects=True, vmem_limit_bytes=48 << 20
-        ),
-        cost_estimate=pl.CostEstimate(
-            flops=40 * length * channels * states, bytes_accessed=16 * length * channels,
-            transcendentals=4 * length * channels * states,
-        ),
-        name="mixer",
-    )(
-        x,
-        raw,
-        dy,
-        bias.reshape(groups, 1, LANES),
-        skip.reshape(groups, 1, LANES),
-        rate_gn,
-        rate_ng,
-        ordered(write),
-        ordered(read),
-    )
-    scale = 1.0 / math.sqrt(length * seq * dp)
-    decay = red[:, :groups].reshape(states, channels).T * scale
-    rows = red[:, groups : groups + 2].reshape(2 * states, LANES) * scale
-    return (
-        y,
-        xg,
-        rg,
-        decay,
-        rows[groups : 2 * groups].reshape(channels),
-        rows[:groups].reshape(channels),
-    )
-
-
-def window_kernel(
-    q_ref, k_ref, v_ref, do_ref, kb_ref, vb_ref, doc_col_ref, doc_row_ref,
-    o_ref, dq_ref, dk_ref, dv_ref, dkb_ref, dvb_ref,
-):
-    length, width = q_ref.shape[1:]
-    scale = 1.0 / math.sqrt(HD)
-    query = lax.broadcasted_iota(jnp.int32, (length, 2 * length), 0)
-    key = lax.broadcasted_iota(jnp.int32, (length, 2 * length), 1)
-    offset = query + length - key
-    allowed = (offset >= 0) & (offset < WINDOW) & (doc_row_ref[...] == doc_col_ref[...])
-    for head in range(width // HD):
-        at = slice(head * HD, (head + 1) * HD)
-        q, do = (q_ref[0, :, at], do_ref[0, :, at])
-        k = jnp.concatenate([kb_ref[0, :, at], k_ref[0, :, at]], axis=0)
-        v = jnp.concatenate([vb_ref[0, :, at], v_ref[0, :, at]], axis=0)
-        over_lanes = (((1,), (1,)), ((), ()))
-        over_rows = (((0,), (0,)), ((), ()))
-        plain = (((1,), (0,)), ((), ()))
-        scores = lax.dot_general(q, k, over_lanes, preferred_element_type=F32) * scale
-        scores = jnp.where(allowed, scores, NEG)
-        top = jnp.max(scores, axis=1, keepdims=True)
-        raised = jnp.exp(scores - top)
-        probs = raised / jnp.sum(raised, axis=1, keepdims=True)
-        low = probs.astype(BF16)
-        out = lax.dot_general(low, v, plain, preferred_element_type=F32).astype(BF16)
-        row_term = jnp.sum(do.astype(F32) * out.astype(F32), axis=1, keepdims=True)
-        value_score = lax.dot_general(do, v, over_lanes, preferred_element_type=F32)
-        grad = (probs * (value_score - row_term)).astype(BF16)
-        o_ref[0, :, at] = out
-        dq_ref[0, :, at] = (
-            lax.dot_general(grad, k, plain, preferred_element_type=F32) * scale
-        ).astype(BF16)
-        dk = lax.dot_general(grad, q, over_rows, preferred_element_type=F32) * scale
-        dv = lax.dot_general(low, do, over_rows, preferred_element_type=F32)
-        dkb_ref[0, :, at] = dk[:length].astype(BF16)
-        dvb_ref[0, :, at] = dv[:length].astype(BF16)
-        dk_ref[0, :, at] = dk[length:]
-        dv_ref[0, :, at] = dv[length:]
-
-
-def shifted(value, steps):
-    count = lax.axis_size("seq")
-    leading, last = (max(0, -steps), min(count, count - steps))
-    return lax.ppermute(value, "seq", [(source, source + steps) for source in range(leading, last)])
-
-
-def window(query, key, value, out_grad, docs):
-    length = query.shape[1]
-    doc_now = docs + 1
-    key_before, value_before = (shifted(key, 1), shifted(value, 1))
-    doc_before = shifted(doc_now, 1)
-    doc_row = jnp.concatenate([doc_before, doc_now], axis=1)
-    inside = pl.BlockSpec(memory_space=pltpu.VMEM)
-    wide = jax.ShapeDtypeStruct(query.shape, F32)
-    low = jax.ShapeDtypeStruct(query.shape, BF16)
-    out, dq, dk, dv, dkb, dvb = pl.pallas_call(
-        window_kernel,
-        out_shape=(low, low, wide, wide, low, low),
-        in_specs=[inside] * 8,
-        out_specs=(inside,) * 6,
-        compiler_params=pltpu.CompilerParams(vmem_limit_bytes=48 << 20),
-        cost_estimate=pl.CostEstimate(
-            flops=20 * length * length * query.shape[2],
-            bytes_accessed=24 * length * query.shape[2],
-            transcendentals=0,
-        ),
-        name="window",
-    )(query, key, value, out_grad, key_before, value_before, doc_now.reshape(length, 1), doc_row)
-    dk = dk + shifted(dkb, -1).astype(F32)
-    dv = dv + shifted(dvb, -1).astype(F32)
-    return (out, dq, dk.astype(BF16), dv.astype(BF16))
+
+
+def step_kernel(sizes, seq, dp, names, *refs):
+    groups, states, steps = sizes
+    hbm, (bias_ref, skip_ref, decay_ref, write_ref, read_ref, doc_ref) = (refs[:7], refs[7:13])
+    y_ref, xg_ref, rg_ref, o_ref, dq_ref, dk_ref, dv_ref = refs[13:20]
+    decay_out, skip_out, bias_out = refs[20:23]
+    sc = dict(zip(names, refs[23:]))
+    load_sem, send_sem, recv_sem, halo_send, halo_recv = refs[23 + len(names) :]
+    me = lax.axis_index("seq")
+    row = lax.axis_index("dp")
+
+    loads = [
+        pltpu.make_async_copy(source.at[0], sc[name], load_sem.at[at])
+        for at, (source, name) in enumerate(zip(hbm, ("x", "raw", "dy", "q", "k", "v", "do")))
+    ]
+    for load in loads:
+        load.start()
+    barrier = pltpu.get_barrier_semaphore()
+    for d in range(1, seq):
+        pl.semaphore_signal(
+            barrier, inc=1, device_id={"seq": lax.rem(me + d, seq)}, device_id_type=MESH
+        )
+    for d in range(1, dp):
+        pl.semaphore_signal(
+            barrier, inc=1, device_id={"dp": lax.rem(row + d, dp)}, device_id_type=MESH
+        )
+    for load in loads[:3]:
+        load.wait()
+    prepare(sizes, me, bias_ref, decay_ref, write_ref, read_ref, sc)
+    summarize(sizes, sc)
+    for load in loads[3:]:
+        load.wait()
+    pl.semaphore_wait(barrier, seq + dp - 2)
+
+    def args(stage, axis, count, at, source, landing, slotted):
+        return (
+            axis, count, at, sc[source], sc[landing], send_sem.at[stage], recv_sem.at[stage], slotted
+        )
+
+    def halo(at, source, landing, steps):
+        return pltpu.make_async_remote_copy(
+            src_ref=source,
+            dst_ref=sc[landing],
+            send_sem=halo_send.at[at],
+            recv_sem=halo_recv.at[at],
+            device_id={"seq": lax.rem(me + steps + seq, seq)},
+            device_id_type=MESH,
+        )
+
+    stage = args(0, "seq", seq, me, "send1", "recv1", True)
+    copies = exchange(*stage)
+    ahead = [
+        halo(0, sc["k"], "k_in", 1),
+        halo(1, sc["v"], "v_in", 1),
+        halo(2, doc_ref, "doc_in", 1),
+    ]
+    for copy in ahead:
+        copy.start()
+    arrivals(*stage)
+    starts(seq, me, sc)
+    stage = args(1, "seq", seq, me, "send2", "recv2", True)
+    copies += exchange(*stage)
+    for copy in ahead:
+        copy.wait_recv()
+    window(me == 0, o_ref, dq_ref, doc_ref, sc)
+    behind = [halo(3, sc["dk_out"], "dk_in", -1), halo(4, sc["dv_out"], "dv_in", -1)]
+    for copy in behind:
+        copy.start()
+    arrivals(*stage)
+    finish(sizes, skip_ref, y_ref, xg_ref, rg_ref, sc)
+    stage = args(2, "seq", seq, me, "send3", "recv3", True)
+    copies += exchange(*stage)
+    for copy in behind:
+        copy.wait_recv()
+    dk_ref[0] = (sc["dk"][...] + sc["dk_in"][...].astype(F32)).astype(BF16)
+    dv_ref[0] = (sc["dv"][...] + sc["dv_in"][...].astype(F32)).astype(BF16)
+    arrivals(*stage)
+    sc["recv3"][me] = sc["send3"][me]
+    sc["send4"][...] = jnp.sum(sc["recv3"][...].astype(F32), axis=0).astype(BF16)
+    stage = args(3, "dp", dp, row, "send4", "recv4", False)
+    copies += exchange(*stage)
+    arrivals(*stage)
+    sc["recv4"][row] = sc["send4"][...]
+    sc["send5"][...] = jnp.sum(sc["recv4"][...].astype(F32), axis=0).astype(BF16)
+    stage = args(4, "seq", seq, me, "send5", "recv5", False)
+    copies += exchange(*stage)
+    arrivals(*stage)
+    sc["recv5"][me] = sc["send5"][...]
+    scale = 1.0 / math.sqrt(steps * CHUNKS * seq * dp)
+    sc["sums"][...] = sc["recv5"][...].astype(F32) * scale
+    for g in range(groups):
+        lanes = slice(g * LANES, (g + 1) * LANES)
+        decay_out[:, lanes] = sc["sums"][:, g, :]
+        bias_out[:, lanes] = sc["sums"][g // 2, groups + g % 2 : groups + g % 2 + 1, :]
+        h = g + groups
+        skip_out[:, lanes] = sc["sums"][h // 2, groups + h % 2 : groups + h % 2 + 1, :]
+    for copy in copies + ahead + behind:
+        copy.wait_send()
+
+
+def flush_kernel(*refs):
+    count = len(refs) // 2
+    sem = refs[-1]
+    copies = [
+        pltpu.make_async_copy(refs[at], refs[count + at], sem.at[at]) for at in range(count)
+    ]
+    for copy in copies:
+        copy.start()
+    for copy in copies:
+        copy.wait()
 
 
 def body(
@@ -500,11 +499,63 @@
     attn_grad,
     document_id,
 ):
-    scanned = mixer(
-        mixer_in, delta_raw, mixer_grad, delta_bias, decay_log, skip_gain, state_write, state_read
+    seq, dp = (lax.axis_size("seq"), lax.axis_size("dp"))
+    _, length, channels = mixer_in.shape
+    width = attn_query.shape[2]
+    states = decay_log.shape[1]
+    sizes = (channels // LANES, states, length // CHUNKS)
+    scratch = scratch_shapes(sizes, length, width, seq, dp)
+    inside = pl.BlockSpec(memory_space=pltpu.VMEM)
+    outside = pl.BlockSpec(memory_space=pltpu.HBM)
+    shapes = (
+        [jax.ShapeDtypeStruct(mixer_in.shape, BF16)] * 3
+        + [jax.ShapeDtypeStruct(attn_query.shape, BF16)] * 4
+        + [jax.ShapeDtypeStruct((states, channels), F32)]
+        + [jax.ShapeDtypeStruct((1, channels), F32)] * 2
     )
-    attended = window(attn_query, attn_key, attn_value, attn_grad, document_id)
-    return scanned + attended
+    results = pl.pallas_call(
+        functools.partial(step_kernel, sizes, seq, dp, tuple(scratch)),
+        out_shape=tuple(shapes),
+        in_specs=[outside] * 7 + [inside] * 6,
+        out_specs=(inside,) * len(shapes),
+        scratch_shapes=[pltpu.VMEM(*shape) for shape in scratch.values()]
+        + [
+            pltpu.SemaphoreType.DMA((7,)),
+            pltpu.SemaphoreType.DMA((5, seq)),
+            pltpu.SemaphoreType.DMA((5, seq)),
+            pltpu.SemaphoreType.DMA((5,)),
+            pltpu.SemaphoreType.DMA((5,)),
+        ],
+        compiler_params=pltpu.CompilerParams(
+            collective_id=0, has_side_effects=True, vmem_limit_bytes=48 << 20
+        ),
+        name="step",
+    )(
+        pltpu.with_memory_space_constraint(mixer_in, pltpu.HBM),
+        pltpu.with_memory_space_constraint(delta_raw, pltpu.HBM),
+        pltpu.with_memory_space_constraint(mixer_grad, pltpu.HBM),
+        pltpu.with_memory_space_constraint(attn_query, pltpu.HBM),
+        pltpu.with_memory_space_constraint(attn_key, pltpu.HBM),
+        pltpu.with_memory_space_constraint(attn_value, pltpu.HBM),
+        pltpu.with_memory_space_constraint(attn_grad, pltpu.HBM),
+        delta_bias.reshape(1, channels),
+        skip_gain.reshape(1, channels),
+        decay_log.T,
+        state_write.transpose(0, 2, 1),
+        state_read.transpose(0, 2, 1),
+        document_id,
+    )
+    results = pl.pallas_call(
+        flush_kernel,
+        out_shape=tuple(shapes),
+        in_specs=[inside] * len(shapes),
+        out_specs=(outside,) * len(shapes),
+        scratch_shapes=[pltpu.SemaphoreType.DMA((len(shapes),))],
+        compiler_params=pltpu.CompilerParams(vmem_limit_bytes=1 << 20),
+        name="flush",
+    )(*results)
+    y, xg, rg, o, dq, dk, dv, decay, skip, bias = results
+    return (y, xg, rg, decay.T, skip.reshape(channels), bias.reshape(channels), o, dq, dk, dv)
 
 
 def solution(mesh):

time: 136 us -> 117 us (0.86)
  starting transfers between devices: 20.7 us -> 0 us
  Pallas kernels: 98.1 us -> 112 us
  waiting for transfers between devices: 6.22 us -> 0 us
  local copies, waits for them, and re-layouts: 6.85 us -> 2.28 us
  other arithmetic: 3.02 us -> 1.24 us
    ppermute x5 -> x0, starting transfers between devices: 20.7 us -> none  [shifted(): lax.ppermute(value, 'seq', [(source, source + steps) for source in range(...]
    pallas_call x2, Pallas kernels: 98.1 us -> 112 us  [the longest x1 111 us: body(): pl.pallas_call(functools.partial(step_kernel, sizes, seq, dp, tuple(scrat...]
    ppermute x5 -> x0, waiting for transfers between devices: 6.22 us -> none  [shifted(): lax.ppermute(value, 'seq', [(source, source + steps) for source in range(...]
    unnamed x26 -> x10, local copies, waits for them, and re-layouts: 5.1 us -> 1.57 us
    convert_element_type x2 -> x0, other arithmetic: 1.42 us -> none  [window(): return (out, dq, dk.astype(BF16), dv.astype(BF16))]
  transfers between devices with their start and end apart: 5 -> 0, of which waited for: 2 -> 0; matrix products, arithmetic and copies ran while one was open for 3% -> 0% of each run, Pallas kernels for 67% -> 0%
where the time goes in v2:
time: 117 us
  Pallas kernels  112 us (96%)
  local copies, waits for them, and re-layouts  2.28 us (2%)
  other arithmetic  1.24 us (1%)
    pallas_call x1, Pallas kernels, body(): pl.pallas_call(functools.partial(step_kernel, sizes, seq, dp, tuple(scrat...  111 us

profile of v2, /device:TPU:80, one launch (start us, length us, event | category | flops | bytes accessed | tf_op | source)
XLA Modules:
  0.0 116.6 jit_solution(12246477824511420804)
XLA Ops:
  0.6 0.0 copy-start.4
  0.7 0.7 reshape.32.refs_7_
  1.4 0.0 copy-done.4
  1.4 0.0 copy-start.1
  1.4 0.0 copy-start.2
  1.4 0.0 copy-start.3
  1.4 0.6 copy-done.1
  2.1 0.0 copy-done.2
  2.1 0.0 copy-done.3
  2.1 0.0 copy-start
  2.1 0.9 copy-done
  3.0 111.0 %step.1 = (bf16[1,128,1536]{2,1,0:T(8,128)(2,1)S(1)}, bf16[1,128,1536]{2,1,0:T(8,128)(2,1)S(1)}, bf16[1,128,1536]{2,1,0:T(8,128)(2,1)S(1)}, bf16[1,128,768]{2,1,...) custom-call(bf16[1,128,1536]{2,1,0:T(8,128)(2,1)} %refs_0_.1, ...), custom_call_target="tpu_custom_call" | custom-call | tf_op jit(solution)/shard_map/step/pallas_call | solution.py:516
  114.0 1.4 %flush.1 = (bf16[1,128,1536]{2,1,0:T(8,128)(2,1)}, bf16[1,128,1536]{2,1,0:T(8,128)(2,1)}, bf16[1,128,1536]{2,1,0:T(8,128)(2,1)}, bf16[1,128,768]{2,1,0:T(8,128)(...) custom-call(bf16[1,128,1536]{2,1,0:T(8,128)(2,1)S(1)} %get-tuple-ele, ...), custom_call_target="tpu_custom_call" | custom-call | tf_op jit(solution)/shard_map/flush/pallas_call | solution.py:548
  115.4 0.6 reduce
  116.0 0.6 reduce.1
  (1 shorter events, 0.0 us)
Async XLA Ops:
  0.6 0.7 copy-start.4
  1.4 0.7 copy-start.1
  1.4 0.7 copy-start.2
  1.4 0.7 copy-start.3
  2.1 0.9 copy-start

commit v3 on v2

v3 whole, which is shorter than its diff:
```python
import functools
import math
import types

import jax
import jax.numpy as jnp
from jax import lax
from jax.experimental import pallas as pl
from jax.experimental.pallas import tpu as pltpu
from jax.sharding import PartitionSpec as P

HD = 96
WINDOW = 128
CHUNKS = 8
LANES = 128
BLOCK = 8
SMALL = 4
NEG = -1e30
BIG = 1e30
LOG2E = math.log2(math.e)
LN2 = math.log(2.0)
MESH = pl.DeviceIdType.MESH
F32 = jnp.float32
BF16 = jnp.bfloat16


def by_distance(count):
    return sorted(range(1, count), key=lambda d: -min(d, count - d))


def exchange(axis, count, me, source, landing, send_sem, recv_sem, slotted):
    copies = []
    for d in by_distance(count):
        peer = lax.rem(me + d, count)
        copy = pltpu.make_async_remote_copy(
            src_ref=source.at[peer] if slotted else source,
            dst_ref=landing.at[me],
            send_sem=send_sem.at[d],
            recv_sem=recv_sem.at[me],
            device_id={axis: peer},
            device_id_type=MESH,
        )
        copy.start()
        copies.append(copy)
    return copies


def arrivals(axis, count, me, source, landing, send_sem, recv_sem, slotted, origins):
    for j in origins:

        @pl.when(me != j)
        def _():
            pltpu.make_async_remote_copy(
                src_ref=source.at[j] if slotted else source,
                dst_ref=landing.at[j],
                send_sem=send_sem.at[0],
                recv_sem=recv_sem.at[j],
                device_id={axis: j},
                device_id_type=MESH,
            ).wait_recv()


def tree(terms):
    while len(terms) > 1:
        terms = [
            terms[at] + terms[at + 1] if at + 1 < len(terms) else terms[at]
            for at in range(0, len(terms), 2)
        ]
    return terms[0]


def shifted_rows(value, steps):
    return pltpu.roll(value, steps % CHUNKS, 0)


def prepare(sizes, arrived, sc):
    groups, states, steps = sizes
    rate = -LOG2E * jnp.exp(sc.decay[...])
    sc.lined[...] = jnp.zeros(sc.lined.shape, F32)
    for g in range(groups):
        sc.rate[g] = rate[:, g * LANES : (g + 1) * LANES]
        sc.lined[:, g] = rate[:, g * LANES : (g + 1) * LANES]
    for ref in (sc.coef, sc.rows):
        ref[...] = jnp.zeros(ref.shape, F32)
    for source, wide in ((sc.write, sc.wb), (sc.read, sc.rb)):
        sc.nat[0, :, 0:states] = source[0].astype(F32).T
        for i in range(steps):
            rows = sc.nat.at[0][pl.ds(i, CHUNKS, stride=steps), :]
            for n in range(states):
                wide[i, n] = jnp.broadcast_to(rows[:, n : n + 1], (CHUNKS, LANES))
    arrived()

    def one(g, carry):
        lanes = pl.ds(pl.multiple_of(g * LANES, LANES), LANES)
        z = sc.raw[:, lanes].astype(F32) + sc.bias[:, lanes]
        small = jnp.exp(-jnp.abs(z))
        step = jnp.maximum(z, 0.0) + jnp.log(1.0 + small)
        sig = jnp.where(z >= 0, 1.0, small) / (1.0 + small)
        for at, value in enumerate(
            (step, sig, sc.x[:, lanes].astype(F32), sc.dy[:, lanes].astype(F32))
        ):
            sc.nat[at] = value
            for i in range(steps):
                sc.items[at, g, i] = sc.nat.at[at][pl.ds(i, CHUNKS, stride=steps), :]
        return carry

    lax.fori_loop(0, groups, one, 0)


def summarize(sizes, sc):
    groups, states, steps = sizes
    chunk = lax.broadcasted_iota(jnp.int32, (CHUNKS, LANES), 0)

    def one(g, carry):
        total = sc.items[0, g, 0]
        for i in range(1, steps):
            total = total + sc.items[0, g, i]
        ahead, behind = ({1: total}, {1: total})
        for d in (1, 2, 4):
            ahead[2 * d] = ahead[d] + jnp.where(chunk >= d, shifted_rows(ahead[d], d), 0.0)
            behind[2 * d] = behind[d] + jnp.where(
                chunk < CHUNKS - d, shifted_rows(behind[d], -d), 0.0
            )
        sc.before[g] = ahead[8] - total
        sc.after[g] = behind[8] - total
        whole = ahead[8][CHUNKS - 1 : CHUNKS]
        ahead = {d: jnp.where(chunk >= d, ahead[d], BIG) for d in (1, 2, 4)}
        behind = {d: jnp.where(chunk < CHUNKS - d, behind[d], BIG) for d in (1, 2, 4)}

        for block in range(0, states, BLOCK):
            rate = [
                jnp.broadcast_to(sc.rate[g, n : n + 1, :], (CHUNKS, LANES))
                for n in range(block, block + BLOCK)
            ]

            def lap(i, state):
                ending, leading, through = state
                size = sc.items[0, g, i]
                weight = size * sc.items[2, g, i]
                out = sc.items[3, g, i]
                new_e, new_l, new_t = ([], [], [])
                for k in range(BLOCK):
                    decay = jnp.exp2(rate[k] * size)
                    passed = through[k] * decay
                    new_e.append(decay * ending[k] + weight * sc.wb[i, block + k])
                    new_l.append(leading[k] + passed * (out * sc.rb[i, block + k]))
                    new_t.append(passed)
                return (tuple(new_e), tuple(new_l), tuple(new_t))

            zero = jnp.zeros((CHUNKS, LANES), F32)
            ending, leading, _ = lax.fori_loop(
                0,
                steps,
                lap,
                ((zero,) * BLOCK, (zero,) * BLOCK, (jnp.ones((CHUNKS, LANES), F32),) * BLOCK),
                unroll=16,
            )
            for k in range(BLOCK):
                n = block + k
                e, b = (ending[k], leading[k])
                for d in (1, 2, 4):
                    e = e + jnp.exp2(rate[k] * ahead[d]) * shifted_rows(e, d)
                    b = b + jnp.exp2(rate[k] * behind[d]) * shifted_rows(b, -d)
                sc.chunk_e[g, n] = e
                sc.chunk_b[g, n] = b
                sc.wide[n, pl.ds(g, 1), :] = e[CHUNKS - 1 : CHUNKS]
                sc.wide[n, pl.ds(16 + g, 1), :] = b[0:1]
                sc.wide[n, pl.ds(32 + g, 1), :] = whole
        return carry

    sc.wide[...] = jnp.zeros(sc.wide.shape, F32)
    lax.fori_loop(0, groups, one, 0)
    sc.send1[...] = sc.wide[...].astype(BF16)


def forward_starts(count, me, sc):
    sc.recv1[me] = sc.send1[me]
    rate = sc.lined[me]
    state = jnp.zeros((16, LANES), F32)
    for j in range(count):
        sc.send2[j] = state.astype(BF16)
        if j + 1 < count:
            ending = sc.recv1[j, 0:16].astype(F32)
            total = sc.recv1[j, 32:48].astype(F32)
            state = jnp.exp2(rate * total) * state + ending
    sc.recv2[me] = sc.send2[me]


def backward_starts(count, me, sc):
    rate = sc.lined[me]
    back = jnp.zeros((16, LANES), F32)
    for j in reversed(range(count)):
        sc.send6[j] = back.astype(BF16)
        if j > 0:
            leading = sc.recv1[j, 16:32].astype(F32)
            total = sc.recv1[j, 32:48].astype(F32)
            back = jnp.exp2(rate * total) * back + leading
    sc.recv6[me] = sc.send6[me]


def coefficients(sizes, sc):
    groups, states, steps = sizes
    chunk = lax.broadcasted_iota(jnp.int32, (CHUNKS, LANES), 0)
    zero = jnp.zeros((CHUNKS, LANES), F32)

    def total(value):
        return jnp.sum(value, axis=0, keepdims=True)

    def one(g, carry):
        bias_sum, skip_sum, sig_sum = (zero, zero, zero)
        for i in range(steps):
            skip_sum = skip_sum + sc.items[2, g, i] * sc.items[3, g, i]
            sig_sum = sig_sum + sc.items[1, g, i]
        sc.rows[1, pl.ds(g, 1), :] = total(skip_sum)
        sc.rows[2, pl.ds(g, 1), :] = total(sig_sum)
        before, after = (sc.before[g], sc.after[g])
        for block in range(0, states, SMALL):
            rate, state, back, through, beyond = ([], [], [], [], [])
            for n in range(block, block + SMALL):
                r = jnp.broadcast_to(sc.rate[g, n : n + 1, :], (CHUNKS, LANES))
                rate.append(r)
                state.append(
                    jnp.where(chunk >= 1, shifted_rows(sc.chunk_e[g, n], 1), 0.0)
                )
                back.append(
                    jnp.where(chunk < CHUNKS - 1, shifted_rows(sc.chunk_b[g, n], -1), 0.0)
                )
                through.append(jnp.exp2(r * before))
                beyond.append(jnp.exp2(r * after))

            def ahead(i, carry):
                h, p = carry
                size = sc.items[0, g, i]
                weight = size * sc.items[2, g, i]
                new_h, new_p = ([], [])
                for k in range(SMALL):
                    decay = jnp.exp2(rate[k] * size)
                    moved = decay * h[k]
                    passed = decay * p[k]
                    sc.moved[i, k] = moved
                    sc.passed[i, k] = passed
                    new_h.append(moved + weight * sc.wb[i, block + k])
                    new_p.append(passed)
                return (tuple(new_h), tuple(new_p))

            lax.fori_loop(0, steps, ahead, (tuple(state), tuple(through)), unroll=16)

            def retreat(lap, carry):
                back, beyond, sums = carry
                i = steps - 1 - lap
                size, sig = (sc.items[0, g, i], sc.items[1, g, i])
                scaled = sig * sc.items[2, g, i]
                out = sc.items[3, g, i]
                new_b, new_q, new_s = ([], [], [])
                for k in range(SMALL):
                    grown = rate[k] * size
                    decay = jnp.exp2(grown)
                    moved, passed = (sc.moved[i, k], sc.passed[i, k])
                    write = scaled * sc.wb[i, block + k]
                    adjoint = out * sc.rb[i, block + k] + back[k]
                    steep = adjoint * grown
                    gated = adjoint * sig
                    far = beyond[k] * moved
                    terms = (
                        moved * steep,
                        passed * steep,
                        far * grown,
                        gated * passed,
                        far * sig,
                        beyond[k] * write,
                        adjoint * write,
                        gated * moved,
                    )
                    new_s.append(tuple(a + b for a, b in zip(sums[k], terms)))
                    new_b.append(decay * adjoint)
                    new_q.append(decay * beyond[k])
                return (tuple(new_b), tuple(new_q), tuple(new_s))

            _, _, sums = lax.fori_loop(
                0,
                steps,
                retreat,
                (tuple(back), tuple(beyond), ((zero,) * 8,) * SMALL),
                unroll=8,
            )
            for k in range(SMALL):
                n = block + k
                slope = LN2 * rate[k]
                kept = (
                    sums[k][0],
                    sums[k][1],
                    sums[k][2],
                    slope * sums[k][3],
                    slope * sums[k][4] + sums[k][5],
                )
                for at, value in enumerate(kept):
                    sc.coef[at, n, pl.ds(g, 1), :] = total(value)
                bias_sum = bias_sum + sums[k][6] + slope * sums[k][7]
        sc.rows[0, pl.ds(g, 1), :] = total(bias_sum)
        return carry

    lax.fori_loop(0, groups, one, 0)


def parameter_sums(sizes, sc):
    groups, states, _ = sizes
    sc.starts[:, 0:16] = sc.recv2[...].astype(F32)
    sc.starts[:, 16:32] = sc.recv6[...].astype(F32)
    whole = sc.wide[0, 32:48]
    bias = sc.rows[0]
    for n in range(states):
        state, back = (sc.starts[n, 0:16], sc.starts[n, 16:32])
        rate = sc.lined[n]
        both = state * back * jnp.exp2(rate * whole)
        sc.sums[n] = LN2 * (
            sc.coef[0, n]
            + state * sc.coef[1, n]
            + back * sc.coef[2, n]
            + both * rate * whole
        )
        bias = bias + (
            state * sc.coef[3, n]
            + back * sc.coef[4, n]
            + both * (LN2 * rate) * sc.rows[2]
        )
    for g in range(groups):
        for at, value in ((g, bias[g : g + 1]), (g + groups, sc.rows[1, g : g + 1])):
            row = groups + at % 2
            sc.sums[at // 2, row : row + 1] = value
    sc.send3[...] = sc.sums[...].astype(BF16)


def finish(sizes, y_ref, xg_ref, rg_ref, sc, low, high):
    groups, states, steps = sizes
    chunk = lax.broadcasted_iota(jnp.int32, (CHUNKS, LANES), 0)

    def one(g, carry):
        lanes = pl.ds(pl.multiple_of(g * LANES, LANES), LANES)
        skip = sc.skip[:, lanes]
        before, after = (sc.before[g], sc.after[g])
        for block in range(0, states, BLOCK):
            rate, state, back = ([], [], [])
            for n in range(block, block + BLOCK):
                r = jnp.broadcast_to(sc.rate[g, n : n + 1, :], (CHUNKS, LANES))
                rate.append(r)
                e = jnp.where(chunk >= 1, shifted_rows(sc.chunk_e[g, n], 1), 0.0)
                b = jnp.where(chunk < CHUNKS - 1, shifted_rows(sc.chunk_b[g, n], -1), 0.0)
                state.append(e + jnp.exp2(r * before) * sc.starts[n, pl.ds(g, 1), :])
                back.append(b + jnp.exp2(r * after) * sc.starts[n, pl.ds(16 + g, 1), :])

            def ahead(i, h):
                size = sc.items[0, g, i]
                weight = size * sc.items[2, g, i]
                if block == 0:
                    mixed = skip * sc.items[2, g, i]
                else:
                    mixed = sc.mixed[i]
                new, terms = ([], [])
                for k in range(BLOCK):
                    moved = jnp.exp2(rate[k] * size) * h[k]
                    sc.moved[i, k] = moved
                    value = moved + weight * sc.wb[i, block + k]
                    terms.append(value * sc.rb[i, block + k])
                    new.append(value)
                sc.mixed[i] = mixed + tree(terms)
                return tuple(new)

            lax.fori_loop(0, steps, ahead, tuple(state), unroll=16)

            def retreat(lap, back):
                i = steps - 1 - lap
                size = sc.items[0, g, i]
                out = sc.items[3, g, i]
                new_b, one_w, one_t = ([], [], [])
                for k in range(BLOCK):
                    grown = rate[k] * size
                    adjoint = out * sc.rb[i, block + k] + back[k]
                    one_w.append(adjoint * sc.wb[i, block + k])
                    one_t.append(adjoint * sc.moved[i, k] * rate[k])
                    new_b.append(jnp.exp2(grown) * adjoint)
                written, turned = (tree(one_w), tree(one_t))
                if block > 0:
                    written = written + sc.written[i]
                    turned = turned + sc.turned[i]
                sc.written[i] = written
                sc.turned[i] = turned
                return tuple(new_b)

            lax.fori_loop(0, steps, retreat, tuple(back), unroll=16)
        for i in range(steps):
            size, sig = (sc.items[0, g, i], sc.items[1, g, i])
            x, out = (sc.items[2, g, i], sc.items[3, g, i])
            written = sc.written[i]
            rows = pl.ds(i, CHUNKS, stride=steps)
            sc.nat.at[0][rows, :] = sc.mixed[i]
            sc.nat.at[1][rows, :] = written * size + skip * out
            sc.nat.at[2][rows, :] = (x * written + LN2 * sc.turned[i]) * sig
        y_ref[0, :, lanes] = sc.nat[0].astype(BF16)
        xg_ref[0, :, lanes] = sc.nat[1].astype(BF16)
        rg_ref[0, :, lanes] = sc.nat[2].astype(BF16)
        return carry

    lax.fori_loop(low, high, one, 0)


def window(first, o_ref, dq_ref, sc):
    length, width = sc.q.shape
    scale = 1.0 / math.sqrt(HD)
    docs = sc.doc[...]
    before = jnp.where(first, -1, sc.doc_in[...])
    own = jnp.broadcast_to(docs.astype(F32), (length, length)).T
    own = jnp.concatenate([own, own], axis=1)
    seen = jnp.concatenate([before, docs], axis=1).astype(F32)
    query = lax.broadcasted_iota(jnp.int32, (length, 2 * length), 0)
    key = lax.broadcasted_iota(jnp.int32, (length, 2 * length), 1)
    offset = query + length - key
    allowed = (offset >= 0) & (offset < WINDOW) & (own == seen)
    over_lanes = (((1,), (1,)), ((), ()))
    over_rows = (((0,), (0,)), ((), ()))
    plain = (((1,), (0,)), ((), ()))
    for head in range(width // HD):
        at = slice(head * HD, (head + 1) * HD)
        q, do = (sc.q[:, at], sc.do[:, at])
        k = jnp.concatenate([sc.k_in[:, at], sc.k[:, at]], axis=0)
        v = jnp.concatenate([sc.v_in[:, at], sc.v[:, at]], axis=0)
        scores = lax.dot_general(q, k, over_lanes, preferred_element_type=F32) * scale
        scores = jnp.where(allowed, scores, NEG)
        top = jnp.max(scores, axis=1, keepdims=True)
        raised = jnp.exp(scores - top)
        probs = raised / jnp.sum(raised, axis=1, keepdims=True)
        low = probs.astype(BF16)
        out = lax.dot_general(low, v, plain, preferred_element_type=F32).astype(BF16)
        row_term = jnp.sum(do.astype(F32) * out.astype(F32), axis=1, keepdims=True)
        value_score = lax.dot_general(do, v, over_lanes, preferred_element_type=F32)
        grad = (probs * (value_score - row_term)).astype(BF16)
        o_ref[0, :, at] = out
        dq_ref[0, :, at] = (
            lax.dot_general(grad, k, plain, preferred_element_type=F32) * scale
        ).astype(BF16)
        dk = lax.dot_general(grad, q, over_rows, preferred_element_type=F32) * scale
        dv = lax.dot_general(low, do, over_rows, preferred_element_type=F32)
        sc.dk_out[:, at] = dk[:length].astype(BF16)
        sc.dv_out[:, at] = dv[:length].astype(BF16)
        sc.dk[:, at] = dk[length:]
        sc.dv[:, at] = dv[length:]


def scratch_shapes(sizes, length, width, seq, dp):
    groups, states, steps = sizes
    channels = groups * LANES
    grid = (steps, states, CHUNKS, LANES)
    line = (steps, CHUNKS, LANES)
    return dict(
        x=((length, channels), BF16),
        raw=((length, channels), BF16),
        dy=((length, channels), BF16),
        q=((length, width), BF16),
        k=((length, width), BF16),
        v=((length, width), BF16),
        do=((length, width), BF16),
        bias=((1, channels), F32),
        skip=((1, channels), F32),
        decay=((states, channels), F32),
        write=((1, states, length), BF16),
        read=((1, states, length), BF16),
        doc=((1, length), jnp.int32),
        k_in=((length, width), BF16),
        v_in=((length, width), BF16),
        doc_in=((1, length), jnp.int32),
        dk=((length, width), F32),
        dv=((length, width), F32),
        dk_out=((length, width), BF16),
        dv_out=((length, width), BF16),
        dk_in=((length, width), BF16),
        dv_in=((length, width), BF16),
        rate=((groups, states, LANES), F32),
        lined=((states, 16, LANES), F32),
        coef=((5, states, 16, LANES), F32),
        rows=((3, 16, LANES), F32),
        passed=((steps, SMALL, CHUNKS, LANES), F32),
        wb=(grid, F32),
        rb=(grid, F32),
        nat=((4, length, LANES), F32),
        items=((4, groups) + line, F32),
        before=((groups, CHUNKS, LANES), F32),
        after=((groups, CHUNKS, LANES), F32),
        chunk_e=((groups, states, CHUNKS, LANES), F32),
        chunk_b=((groups, states, CHUNKS, LANES), F32),
        wide=((states, 48, LANES), F32),
        send1=((states, 48, LANES), BF16),
        recv1=((seq, 48, LANES), BF16),
        send2=((seq, 16, LANES), BF16),
        recv2=((states, 16, LANES), BF16),
        send6=((seq, 16, LANES), BF16),
        recv6=((states, 16, LANES), BF16),
        starts=((states, 32, LANES), F32),
        sums=((states, 16, LANES), F32),
        moved=((steps, BLOCK, CHUNKS, LANES), F32),
        mixed=(line, F32),
        written=(line, F32),
        turned=(line, F32),
        send3=((states, 16, LANES), BF16),
        recv3=((seq, 16, LANES), BF16),
        send4=((16, LANES), BF16),
        recv4=((dp, 16, LANES), BF16),
        send5=((16, LANES), BF16),
        recv5=((states, 16, LANES), BF16),
    )


def step_kernel(sizes, seq, dp, names, *refs):
    groups, states, steps = sizes
    hbm = refs[:13]
    y_ref, xg_ref, rg_ref, o_ref, dq_ref, dk_ref, dv_ref = refs[13:20]
    decay_out, skip_out, bias_out = refs[20:23]
    sc = types.SimpleNamespace(**dict(zip(names, refs[23:])))
    load_sem, send_sem, recv_sem, halo_send, halo_recv = refs[23 + len(names) :]
    me = lax.axis_index("seq")
    row = lax.axis_index("dp")
    final = seq - 1

    places = [sc.decay, sc.write, sc.read, sc.bias.at[0], sc.skip.at[0], sc.doc]
    places += [sc.x, sc.raw, sc.dy, sc.q, sc.k, sc.v, sc.do]
    loads = [
        pltpu.make_async_copy(source if at < 6 else source.at[0], place, load_sem.at[at])
        for at, (source, place) in enumerate(zip(hbm, places))
    ]
    for load in loads:
        load.start()
    barrier = pltpu.get_barrier_semaphore()
    for d in range(1, seq):
        pl.semaphore_signal(
            barrier, inc=1, device_id={"seq": lax.rem(me + d, seq)}, device_id_type=MESH
        )
    for d in range(1, dp):
        pl.semaphore_signal(
            barrier, inc=1, device_id={"dp": lax.rem(row + d, dp)}, device_id_type=MESH
        )

    def arrived():
        for load in loads[3:9]:
            load.wait()

    for load in loads[:3]:
        load.wait()
    prepare(sizes, arrived, sc)
    summarize(sizes, sc)
    for load in loads[9:]:
        load.wait()
    pl.semaphore_wait(barrier, seq + dp - 2)

    def stage(at, source, landing, slotted):
        return ("seq", seq, me, source, landing, send_sem.at[at], recv_sem.at[at], slotted)

    def halo(at, source, landing, steps):
        return pltpu.make_async_remote_copy(
            src_ref=source,
            dst_ref=landing,
            send_sem=halo_send.at[at],
            recv_sem=halo_recv.at[at],
            device_id={"seq": lax.rem(me + steps + seq, seq)},
            device_id_type=MESH,
        )

    summed = stage(0, sc.send1, sc.recv1, True)
    copies = exchange(*summed)
    ahead = [halo(0, sc.k, sc.k_in, 1), halo(1, sc.v, sc.v_in, 1), halo(2, sc.doc, sc.doc_in, 1)]
    key_back = halo(3, sc.dk_out, sc.dk_in, -1)
    value_back = halo(4, sc.dv_out, sc.dv_in, -1)

    def attend():
        @pl.when(me > 0)
        def _():
            for copy in ahead:
                copy.wait_recv()

        window(me == 0, o_ref, dq_ref, sc)

    @pl.when(me < final)
    def _():
        for copy in ahead:
            copy.start()
        coefficients(sizes, sc)

    @pl.when(me == 0)
    def _():
        sc.k_in[...] = jnp.zeros(sc.k_in.shape, BF16)
        sc.v_in[...] = jnp.zeros(sc.v_in.shape, BF16)
        sc.doc_in[...] = jnp.zeros(sc.doc_in.shape, jnp.int32)

    @pl.when(me == final)
    def _():
        sc.dk_in[...] = jnp.zeros(sc.dk_in.shape, BF16)
        sc.dv_in[...] = jnp.zeros(sc.dv_in.shape, BF16)

    arrivals(*summed, range(final))
    forward_starts(seq, me, sc)
    forward = stage(1, sc.send2, sc.recv2, True)
    copies += exchange(*forward)
    arrivals(*summed, [final])
    backward_starts(seq, me, sc)
    backward = stage(2, sc.send6, sc.recv6, True)
    copies += exchange(*backward)

    @pl.when(me == final)
    def _():
        coefficients(sizes, sc)

    @pl.when(me < final)
    def _():
        attend()

    arrivals(*forward, range(seq))
    arrivals(*backward, range(seq))
    parameter_sums(sizes, sc)
    reduced = stage(3, sc.send3, sc.recv3, True)
    copies += exchange(*reduced)
    late = lax.div(me, final)
    cut = groups * 2 // 3 * (1 - late)
    middle = groups - late * (groups * 7 // 12)
    finished = functools.partial(finish, sizes, y_ref, xg_ref, rg_ref, sc)

    @pl.when(me == final)
    def _():
        attend()

    finished(0, cut)
    arrivals(*reduced, range(seq))
    sc.recv3[me] = sc.send3[me]
    sc.send4[...] = jnp.sum(sc.recv3[...].astype(F32), axis=0).astype(BF16)
    crossed = ("dp", dp, row, sc.send4, sc.recv4, send_sem.at[4], recv_sem.at[4], False)
    copies += exchange(*crossed)

    @pl.when(me > 0)
    def _():
        key_back.start()

    finished(cut, middle)
    arrivals(*crossed, range(dp))
    sc.recv4[row] = sc.send4[...]
    sc.send5[...] = jnp.sum(sc.recv4[...].astype(F32), axis=0).astype(BF16)
    spread = stage(5, sc.send5, sc.recv5, False)
    copies += exchange(*spread)

    @pl.when(me > 0)
    def _():
        value_back.start()

    finished(middle, groups)

    @pl.when(me < final)
    def _():
        key_back.wait_recv()
        value_back.wait_recv()

    dk_ref[0] = (sc.dk[...] + sc.dk_in[...].astype(F32)).astype(BF16)
    dv_ref[0] = (sc.dv[...] + sc.dv_in[...].astype(F32)).astype(BF16)
    arrivals(*spread, range(seq))
    sc.recv5[me] = sc.send5[...]
    scale = 1.0 / math.sqrt(steps * CHUNKS * seq * dp)
    sc.sums[...] = sc.recv5[...].astype(F32) * scale
    for g in range(groups):
        lanes = slice(g * LANES, (g + 1) * LANES)
        decay_out[:, lanes] = sc.sums[:, g, :]
        bias_out[:, lanes] = sc.sums[g // 2, groups + g % 2 : groups + g % 2 + 1, :]
        h = g + groups
        skip_out[:, lanes] = sc.sums[h // 2, groups + h % 2 : groups + h % 2 + 1, :]
    for copy in copies:
        copy.wait_send()

    @pl.when(me < final)
    def _():
        for copy in ahead:
            copy.wait_send()

    @pl.when(me > 0)
    def _():
        key_back.wait_send()
        value_back.wait_send()


def flush_kernel(*refs):
    count = len(refs) // 2
    sem = refs[-1]
    copies = [
        pltpu.make_async_copy(
            refs[at] if at < count - 2 else refs[at].at[0], refs[count + at], sem.at[at]
        )
        for at in range(count)
    ]
    for copy in copies:
        copy.start()
    for copy in copies:
        copy.wait()


def body(
    mixer_in,
    delta_raw,
    delta_bias,
    decay_log,
    skip_gain,
    state_write,
    state_read,
    mixer_grad,
    attn_query,
    attn_key,
    attn_value,
    attn_grad,
    document_id,
):
    seq, dp = (lax.axis_size("seq"), lax.axis_size("dp"))
    _, length, channels = mixer_in.shape
    width = attn_query.shape[2]
    states = decay_log.shape[1]
    sizes = (channels // LANES, states, length // CHUNKS)
    scratch = scratch_shapes(sizes, length, width, seq, dp)
    inside = pl.BlockSpec(memory_space=pltpu.VMEM)
    outside = pl.BlockSpec(memory_space=pltpu.HBM)
    shapes = (
        [jax.ShapeDtypeStruct(mixer_in.shape, BF16)] * 3
        + [jax.ShapeDtypeStruct(attn_query.shape, BF16)] * 4
        + [jax.ShapeDtypeStruct((states, channels), F32)]
        + [jax.ShapeDtypeStruct((1, channels), F32)] * 2
    )
    operands = (
        decay_log.T,
        state_write.transpose(0, 2, 1),
        state_read.transpose(0, 2, 1),
        delta_bias,
        skip_gain,
        document_id,
        mixer_in,
        delta_raw,
        mixer_grad,
        attn_query,
        attn_key,
        attn_value,
        attn_grad,
    )
    results = pl.pallas_call(
        functools.partial(step_kernel, sizes, seq, dp, tuple(scratch)),
        out_shape=tuple(shapes),
        in_specs=[outside] * 13,
        out_specs=(inside,) * len(shapes),
        scratch_shapes=[pltpu.VMEM(*shape) for shape in scratch.values()]
        + [
            pltpu.SemaphoreType.DMA((13,)),
            pltpu.SemaphoreType.DMA((6, seq)),
            pltpu.SemaphoreType.DMA((6, seq)),
            pltpu.SemaphoreType.DMA((5,)),
            pltpu.SemaphoreType.DMA((5,)),
        ],
        compiler_params=pltpu.CompilerParams(
            collective_id=0, has_side_effects=True, vmem_limit_bytes=48 << 20
        ),
        name="step",
    )(*(pltpu.with_memory_space_constraint(value, pltpu.HBM) for value in operands))
    results = pl.pallas_call(
        flush_kernel,
        out_shape=tuple(shapes[:-2]) + (jax.ShapeDtypeStruct((channels,), F32),) * 2,
        in_specs=[inside] * len(shapes),
        out_specs=(outside,) * len(shapes),
        scratch_shapes=[pltpu.SemaphoreType.DMA((len(shapes),))],
        compiler_params=pltpu.CompilerParams(vmem_limit_bytes=1 << 20),
        name="flush",
    )(*results)
    y, xg, rg, o, dq, dk, dv, decay, skip, bias = results
    return (y, xg, rg, decay.T, skip, bias, o, dq, dk, dv)


def solution(mesh):
    spread = P(("member", "dp"), "seq", "mp")
    shared = P(("member", "dp"), "seq", None)
    one = P(("member", "mp"))
    two = P(("member", "mp"), None)
    return jax.shard_map(
        body,
        mesh=mesh,
        in_specs=(
            spread,
            spread,
            one,
            two,
            one,
            shared,
            shared,
            spread,
            spread,
            spread,
            spread,
            spread,
            P(("member", "dp"), "seq"),
        ),
        out_specs=(spread, spread, spread, two, one, one, spread, spread, spread, spread),
        check_vma=False,
    )
```

time: 117 us -> 99.6 us (0.85)
  Pallas kernels: 112 us -> 98.7 us
  local copies, waits for them, and re-layouts: 2.28 us -> 0 us
  other arithmetic: 1.24 us -> 0 us
    pallas_call x1, Pallas kernels: 111 us -> 97.3 us  [body(): pl.pallas_call(functools.partial(step_kernel, sizes, seq, dp, tuple(scrat...]
    unnamed x10 -> x0, local copies, waits for them, and re-layouts: 1.57 us -> none
    pallas_call x2 -> x0, other arithmetic: 1.24 us -> none  [body(): pl.pallas_call(flush_kernel, out_shape=tuple(shapes), in_specs=[inside] *...]
where the time goes in v3:
time: 99.6 us; the launch traced here: 99.5 us
  Pallas kernels  98.7 us (99%)
    pallas_call x1, Pallas kernels, body(): pl.pallas_call(functools.partial(step_kernel, sizes, seq, dp, tuple(scrat...  97.3 us

profile of v3, /device:TPU:80, one launch (start us, length us, event | category | flops | bytes accessed | tf_op | source)
XLA Modules:
  0.0 99.5 jit_solution(4389052191696059923)
XLA Ops:
  0.6 97.3 %step.1 = (bf16[1,128,1536]{2,1,0:T(8,128)(2,1)S(1)}, bf16[1,128,1536]{2,1,0:T(8,128)(2,1)S(1)}, bf16[1,128,1536]{2,1,0:T(8,128)(2,1)S(1)}, bf16[1,128,768]{2,1,...) custom-call(f32[16,1536]{1,0:T(8,128)} %bitcast.4, ...), custom_call_target="tpu_custom_call" | custom-call | tf_op jit(solution)/shard_map/step/pallas_call | solution.py:741
  98.0 1.4 %flush.1 = (bf16[1,128,1536]{2,1,0:T(8,128)(2,1)}, bf16[1,128,1536]{2,1,0:T(8,128)(2,1)}, bf16[1,128,1536]{2,1,0:T(8,128)(2,1)}, bf16[1,128,768]{2,1,0:T(8,128)(...) custom-call(bf16[1,128,1536]{2,1,0:T(8,128)(2,1)S(1)} %get-tuple-ele, ...), custom_call_target="tpu_custom_call" | custom-call | tf_op jit(solution)/shard_map/flush/pallas_call | solution.py:759

commit v4 on v3

--- a/solution.py
+++ b/solution.py
@@ -198,7 +198,7 @@
     sc.recv6[me] = sc.send6[me]
 
 
-def coefficients(sizes, sc):
+def coefficients(sizes, sc, low, high, closing):
     groups, states, steps = sizes
     chunk = lax.broadcasted_iota(jnp.int32, (CHUNKS, LANES), 0)
     zero = jnp.zeros((CHUNKS, LANES), F32)
@@ -260,46 +260,45 @@
                     adjoint = out * sc.rb[i, block + k] + back[k]
                     steep = adjoint * grown
                     gated = adjoint * sig
-                    far = beyond[k] * moved
-                    terms = (
+                    terms = [
                         moved * steep,
                         passed * steep,
-                        far * grown,
                         gated * passed,
-                        far * sig,
-                        beyond[k] * write,
                         adjoint * write,
                         gated * moved,
-                    )
+                    ]
+                    if not closing:
+                        far = beyond[k] * moved
+                        terms += [far * grown, far * sig, beyond[k] * write]
+                        new_q.append(decay * beyond[k])
                     new_s.append(tuple(a + b for a, b in zip(sums[k], terms)))
                     new_b.append(decay * adjoint)
-                    new_q.append(decay * beyond[k])
                 return (tuple(new_b), tuple(new_q), tuple(new_s))
 
             _, _, sums = lax.fori_loop(
                 0,
                 steps,
                 retreat,
-                (tuple(back), tuple(beyond), ((zero,) * 8,) * SMALL),
+                (
+                    tuple(back),
+                    () if closing else tuple(beyond),
+                    ((zero,) * (5 if closing else 8),) * SMALL,
+                ),
                 unroll=8,
             )
             for k in range(SMALL):
                 n = block + k
                 slope = LN2 * rate[k]
-                kept = (
-                    sums[k][0],
-                    sums[k][1],
-                    sums[k][2],
-                    slope * sums[k][3],
-                    slope * sums[k][4] + sums[k][5],
-                )
+                kept = [sums[k][0], sums[k][1], slope * sums[k][2]]
+                if not closing:
+                    kept += [sums[k][5], slope * sums[k][6] + sums[k][7]]
                 for at, value in enumerate(kept):
                     sc.coef[at, n, pl.ds(g, 1), :] = total(value)
-                bias_sum = bias_sum + sums[k][6] + slope * sums[k][7]
+                bias_sum = bias_sum + sums[k][3] + slope * sums[k][4]
         sc.rows[0, pl.ds(g, 1), :] = total(bias_sum)
         return carry
 
-    lax.fori_loop(0, groups, one, 0)
+    lax.fori_loop(low, high, one, 0)
 
 
 def parameter_sums(sizes, sc):
@@ -315,11 +314,11 @@
         sc.sums[n] = LN2 * (
             sc.coef[0, n]
             + state * sc.coef[1, n]
-            + back * sc.coef[2, n]
+            + back * sc.coef[3, n]
             + both * rate * whole
         )
         bias = bias + (
-            state * sc.coef[3, n]
+            state * sc.coef[2, n]
             + back * sc.coef[4, n]
             + both * (LN2 * rate) * sc.rows[2]
         )
@@ -576,11 +575,14 @@
 
         window(me == 0, o_ref, dq_ref, sc)
 
+    late = lax.div(lax.div(4 * me, seq), 3)
+    ready = groups - late * (groups * 5 // 12) - lax.div(me, final) * (groups - groups * 5 // 12)
+
     @pl.when(me < final)
     def _():
         for copy in ahead:
             copy.start()
-        coefficients(sizes, sc)
+        coefficients(sizes, sc, 0, ready, False)
 
     @pl.when(me == 0)
     def _():
@@ -602,11 +604,15 @@
     backward = stage(2, sc.send6, sc.recv6, True)
     copies += exchange(*backward)
 
+    @pl.when(me < final)
+    def _():
+        coefficients(sizes, sc, ready, groups, False)
+
     @pl.when(me == final)
     def _():
-        coefficients(sizes, sc)
-
-    @pl.when(me < final)
+        coefficients(sizes, sc, 0, groups, True)
+
+    @pl.when(late == 0)
     def _():
         attend()
 
@@ -615,12 +621,11 @@
     parameter_sums(sizes, sc)
     reduced = stage(3, sc.send3, sc.recv3, True)
     copies += exchange(*reduced)
-    late = lax.div(me, final)
     cut = groups * 2 // 3 * (1 - late)
     middle = groups - late * (groups * 7 // 12)
     finished = functools.partial(finish, sizes, y_ref, xg_ref, rg_ref, sc)
 
-    @pl.when(me == final)
+    @pl.when(late == 1)
     def _():
         attend()
 

time: 99.6 us -> 99.2 us (level)
  no operation moved by 1% of the time
where the time goes in v4:
time: 99.2 us; the launch traced here: 99.1 us
  Pallas kernels  98.3 us (99%)
    pallas_call x1, Pallas kernels, body(): pl.pallas_call(functools.partial(step_kernel, sizes, seq, dp, tuple(scrat...  96.9 us

profile of v4, /device:TPU:80, one launch (start us, length us, event | category | flops | bytes accessed | tf_op | source)
XLA Modules:
  0.0 99.1 jit_solution(11271101804455351544)
XLA Ops:
  0.6 96.9 %step.1 = (bf16[1,128,1536]{2,1,0:T(8,128)(2,1)S(1)}, bf16[1,128,1536]{2,1,0:T(8,128)(2,1)S(1)}, bf16[1,128,1536]{2,1,0:T(8,128)(2,1)S(1)}, bf16[1,128,768]{2,1,...) custom-call(f32[16,1536]{1,0:T(8,128)} %bitcast.4, ...), custom_call_target="tpu_custom_call" | custom-call | tf_op jit(solution)/shard_map/step/pallas_call | solution.py:746
  97.5 1.4 %flush.1 = (bf16[1,128,1536]{2,1,0:T(8,128)(2,1)}, bf16[1,128,1536]{2,1,0:T(8,128)(2,1)}, bf16[1,128,1536]{2,1,0:T(8,128)(2,1)}, bf16[1,128,768]{2,1,0:T(8,128)(...) custom-call(bf16[1,128,1536]{2,1,0:T(8,128)(2,1)S(1)} %get-tuple-ele, ...), custom_call_target="tpu_custom_call" | custom-call | tf_op jit(solution)/shard_map/flush/pallas_call | solution.py:764

commit v5 on v4

--- a/solution.py
+++ b/solution.py
@@ -326,7 +326,7 @@
         for at, value in ((g, bias[g : g + 1]), (g + groups, sc.rows[1, g : g + 1])):
             row = groups + at % 2
             sc.sums[at // 2, row : row + 1] = value
-    sc.send3[...] = sc.sums[...].astype(BF16)
+    sc.send3[...] = sc.sums[...].astype(BF16).reshape(sc.send3.shape)
 
 
 def finish(sizes, y_ref, xg_ref, rg_ref, sc, low, high):
@@ -498,12 +498,12 @@
         mixed=(line, F32),
         written=(line, F32),
         turned=(line, F32),
-        send3=((states, 16, LANES), BF16),
-        recv3=((seq, 16, LANES), BF16),
-        send4=((16, LANES), BF16),
-        recv4=((dp, 16, LANES), BF16),
-        send5=((16, LANES), BF16),
-        recv5=((states, 16, LANES), BF16),
+        send3=((dp, states // dp, 16, LANES), BF16),
+        recv3=((dp, states // dp, 16, LANES), BF16),
+        send4=((states // dp, 16, LANES), BF16),
+        recv4=((seq, states // dp, 16, LANES), BF16),
+        send5=((states // dp, 16, LANES), BF16),
+        recv5=((dp, states // dp, 16, LANES), BF16),
     )
 
 
@@ -619,32 +619,39 @@
     arrivals(*forward, range(seq))
     arrivals(*backward, range(seq))
     parameter_sums(sizes, sc)
-    reduced = stage(3, sc.send3, sc.recv3, True)
+    def across(at, source, landing, slotted):
+        return ("dp", dp, row, source, landing, send_sem.at[at], recv_sem.at[at], slotted)
+
+    reduced = across(3, sc.send3, sc.recv3, True)
     copies += exchange(*reduced)
-    cut = groups * 2 // 3 * (1 - late)
-    middle = groups - late * (groups * 7 // 12)
+    cut = groups * 5 // 12 * (1 - late)
+    middle = groups - late * (groups // 3)
     finished = functools.partial(finish, sizes, y_ref, xg_ref, rg_ref, sc)
 
+    @pl.when(me * (1 - late) > 0)
+    def _():
+        key_back.start()
+
     @pl.when(late == 1)
     def _():
         attend()
 
     finished(0, cut)
-    arrivals(*reduced, range(seq))
-    sc.recv3[me] = sc.send3[me]
+    arrivals(*reduced, range(dp))
+    sc.recv3[row] = sc.send3[row]
     sc.send4[...] = jnp.sum(sc.recv3[...].astype(F32), axis=0).astype(BF16)
-    crossed = ("dp", dp, row, sc.send4, sc.recv4, send_sem.at[4], recv_sem.at[4], False)
+    crossed = stage(4, sc.send4, sc.recv4, False)
     copies += exchange(*crossed)
 
-    @pl.when(me > 0)
+    @pl.when(late == 1)
     def _():
         key_back.start()
 
     finished(cut, middle)
-    arrivals(*crossed, range(dp))
-    sc.recv4[row] = sc.send4[...]
+    arrivals(*crossed, range(seq))
+    sc.recv4[me] = sc.send4[...]
     sc.send5[...] = jnp.sum(sc.recv4[...].astype(F32), axis=0).astype(BF16)
-    spread = stage(5, sc.send5, sc.recv5, False)
+    spread = across(5, sc.send5, sc.recv5, False)
     copies += exchange(*spread)
 
     @pl.when(me > 0)
@@ -660,10 +667,10 @@
 
     dk_ref[0] = (sc.dk[...] + sc.dk_in[...].astype(F32)).astype(BF16)
     dv_ref[0] = (sc.dv[...] + sc.dv_in[...].astype(F32)).astype(BF16)
-    arrivals(*spread, range(seq))
-    sc.recv5[me] = sc.send5[...]
+    arrivals(*spread, range(dp))
+    sc.recv5[row] = sc.send5[...]
     scale = 1.0 / math.sqrt(steps * CHUNKS * seq * dp)
-    sc.sums[...] = sc.recv5[...].astype(F32) * scale
+    sc.sums[...] = sc.recv5[...].astype(F32).reshape(sc.sums.shape) * scale
     for g in range(groups):
         lanes = slice(g * LANES, (g + 1) * LANES)
         decay_out[:, lanes] = sc.sums[:, g, :]

time: 99.2 us -> 98.3 us (level)
  Pallas kernels: 98.3 us -> 97.3 us
where the time goes in v5:
time: 98.3 us; the launch traced here: 98.1 us
  Pallas kernels  97.3 us (99%)
    pallas_call x1, Pallas kernels, body(): pl.pallas_call(functools.partial(step_kernel, sizes, seq, dp, tuple(scrat...  95.9 us

profile of v5, /device:TPU:80, one launch (start us, length us, event | category | flops | bytes accessed | tf_op | source)
XLA Modules:
  0.0 98.1 jit_solution(9579457191337861939)
XLA Ops:
  0.6 95.9 %step.1 = (bf16[1,128,1536]{2,1,0:T(8,128)(2,1)S(1)}, bf16[1,128,1536]{2,1,0:T(8,128)(2,1)S(1)}, bf16[1,128,1536]{2,1,0:T(8,128)(2,1)S(1)}, bf16[1,128,768]{2,1,...) custom-call(f32[16,1536]{1,0:T(8,128)} %bitcast.4, ...), custom_call_target="tpu_custom_call" | custom-call | tf_op jit(solution)/shard_map/step/pallas_call | solution.py:753
  96.6 1.4 %flush.1 = (bf16[1,128,1536]{2,1,0:T(8,128)(2,1)}, bf16[1,128,1536]{2,1,0:T(8,128)(2,1)}, bf16[1,128,1536]{2,1,0:T(8,128)(2,1)}, bf16[1,128,768]{2,1,0:T(8,128)(...) custom-call(bf16[1,128,1536]{2,1,0:T(8,128)(2,1)S(1)} %get-tuple-ele, ...), custom_call_target="tpu_custom_call" | custom-call | tf_op jit(solution)/shard_map/flush/pallas_call | solution.py:771
